TPU v7x, 32 devices: a whole 2x2x4 slice. The times are simulated.
32 devices in a mesh: shard: 8 (over z, x), grp: 4 (over y, core).
Axes of the slice: x: 2, y: 2, z: 4, core: 2. Of those that a mesh axis runs over, the one named last changes fastest.
Arguments:
- table_t: bfloat16 [100, 622592], P(None, ('shard', 'grp')), may hold values from -6 to 6
- req_rows: int32 [1024, 128], P(('shard', 'grp')), may hold values from 0 to 19455
- count1: int32 [1024], P(('shard', 'grp')), may hold values from 1 to 128, as said below
- frontier_list: int32 [11, 32768], P(None, ('shard', 'grp')), may hold values from 0 to 4095, as said below
- req2_rows: int32 [1024, 128], P(('shard', 'grp')), may hold values from 0 to 1023
- count2: int32 [1024], P(('shard', 'grp')), may hold values from 1 to 128, as said below
- seed_list: int32 [16, 8192], P(None, ('shard', 'grp')), may hold values from 0 to 4095, as said below
- w1_self: bfloat16 [256, 100], replicated, may hold values from -0.625 to 0.625
- w1_neigh: bfloat16 [256, 100], replicated, may hold values from -1.25 to 1.25
- bias1: float32 [256], replicated, may hold values from -3 to 3
- w2_self: bfloat16 [47, 256], replicated, may hold values from -0.375 to 0.375
- w2_neigh: bfloat16 [47, 256], replicated, may hold values from -0.75 to 0.75
- bias2: float32 [47], replicated, may hold values from -3 to 3
Outputs:
- logits: float32 [47, 8192], P(None, ('shard', 'grp'))
Inputs may be any that keep to these rules, and one draw needn't show every extreme that they name: count1[r * 32 + o] counts the live slots of the block that device r asks of device o; in every draw some devices are asked for 128 rows by every device. `frontier_list`: every entry o * 128 + j names a live slot (j below count1 of that block) of the asking device. count2[r * 32 + o] counts the live slots of the block that device r asks of device o; in every draw some devices are asked for 128 rows by every device. `seed_list`: every entry o * 128 + j names a live slot (j below count2 of that block) of the asking device.
All inputs are finite; a program needn't handle non-finite values.
Results may differ from a plain program's by a relative error of at most 0.0029.
Values may be sent and summed in bfloat16 or wider, within the bound.
A program may use at most 64 MiB of HBM per device.

v0:
```python
import functools

import jax
import jax.numpy as jnp
from jax import lax
from jax.experimental import pallas as pl
from jax.experimental.pallas import tpu as pltpu
from jax.sharding import PartitionSpec as P

AXES = ("shard", "grp")
LANES = 128
MIB = 1024 * 1024
MATRIX_LIMIT = 4 * MIB
VMEM_ALL = pl.BlockSpec(memory_space=pltpu.VMEM)
SMEM_ALL = pl.BlockSpec(memory_space=pltpu.SMEM)


def tall(row, span):
    few = jnp.broadcast_to(row, (16, row.shape[1])).astype(jnp.bfloat16)
    return jnp.concatenate([few] * (span // 16), axis=0)


def local_rows(values, base, span):
    local = values - base
    inside = jnp.logical_and(local >= 0, local < span)
    return jnp.where(inside, local, -1).astype(jnp.float32)


def hits(row, span):
    ids = lax.broadcasted_iota(jnp.int32, (span, row.shape[1]), 0)
    ids = ids.astype(jnp.float32).astype(jnp.bfloat16)
    return jnp.where(tall(row, span) == ids, jnp.ones((), jnp.bfloat16), jnp.zeros((), jnp.bfloat16))


def tile(i, size=LANES):
    return pl.ds(pl.multiple_of(i * size, size), size)


def count_slots(list_ref, own_ref, near_ref, cap, first, last):
    entries, nodes = list_ref.shape
    across = nodes // LANES

    def one(i, carry):
        owner, cols = i // across, tile(i % across)
        at = tile(owner, cap)
        local = local_rows(list_ref[:, cols], owner * cap, cap)
        own_ref[at, cols] = hits(local[0:1], cap)
        total = hits(local[1:2], cap)
        for k in range(2, entries):
            total = total + hits(local[k : k + 1], cap)
        near_ref[at, cols] = total
        return carry

    lax.fori_loop(first * across, last * across, one, 0)


def onehot_slots(ids_ref, out_ref):
    nodes = out_ref.shape[0]
    devices, _, cap = ids_ref.shape

    def one(asker, carry):
        wanted = ids_ref[asker]
        for b in range(nodes // LANES):
            out_ref[b * LANES : (b + 1) * LANES, tile(asker, cap)] = hits(
                local_rows(wanted, b * LANES, LANES), LANES
            )
        return carry

    lax.fori_loop(0, devices, one, 0)


def lay_side_by_side(counts_ref, blocks_ref, flat):
    devices, width, cap = blocks_ref.shape
    slot = lax.broadcasted_iota(jnp.int32, (width, cap), 1)

    def one(o, carry):
        live = jnp.where(slot < counts_ref[o], blocks_ref[o].astype(jnp.float32), 0.0)
        flat[:, tile(o, cap)] = live.astype(jnp.bfloat16)
        return carry

    lax.fori_loop(0, devices, one, 0)


def dot32(a, b):
    return jnp.dot(a, b, preferred_element_type=jnp.float32)


def whole_kernel(
    grp,
    table_ref,
    req_ref,
    req2_ref,
    count1_ref,
    count2_ref,
    front_ref,
    seed_ref,
    w1s_ref,
    w1n_ref,
    bias1_ref,
    w2s_ref,
    w2n_ref,
    out_ref,
    table,
    w1s,
    w1n,
    w2,
    asked,
    asked2,
    ids,
    rows,
    block,
    send,
    got,
    own,
    near,
    onehot,
    seed_own,
    seed_near,
    flat,
    payload,
    send2,
    got2,
    flat2,
    local_sem,
    table_sem,
    sems,
):
    devices, _, cap = req_ref.shape
    me = lax.axis_index(AXES[0]) * grp + lax.axis_index(AXES[1])

    def partner(t):
        return (me + t) % devices

    def copy(what, src, dst, peer):
        return pltpu.make_async_remote_copy(
            src_ref=src.at[peer],
            dst_ref=dst.at[me],
            send_sem=sems.at[2 * what, peer],
            recv_sem=sems.at[2 * what + 1, me],
            device_id=(peer // grp, peer % grp),
            device_id_type=pl.DeviceIdType.MESH,
        )

    def wait_all(what, src, dst):
        def one(t, carry):
            peer = partner(t)
            pltpu.make_async_remote_copy(
                src_ref=src.at[peer],
                dst_ref=dst.at[peer],
                send_sem=sems.at[2 * what, peer],
                recv_sem=sems.at[2 * what + 1, peer],
                device_id=(peer // grp, peer % grp),
                device_id_type=pl.DeviceIdType.MESH,
            ).wait()
            return carry

        lax.fori_loop(1, devices, one, 0)

    load = pltpu.make_async_copy(table_ref, table, table_sem)
    load.start()
    barrier = pltpu.get_barrier_semaphore()

    def greet(t, carry):
        peer = partner(t)
        pl.semaphore_signal(
            barrier,
            inc=1,
            device_id=(peer // grp, peer % grp),
            device_id_type=pl.DeviceIdType.MESH,
        )
        return carry

    lax.fori_loop(1, devices, greet, 0)
    early = devices // 8
    count_slots(front_ref, own, near, cap, 0, early)
    pl.semaphore_wait(barrier, devices - 1)

    def ask(t, carry):
        copy(0, req_ref, asked, partner(t)).start()
        copy(1, req2_ref, asked2, partner(t)).start()
        return carry

    lax.fori_loop(1, devices, ask, 0)
    asked[me] = req_ref[me]
    asked2[me] = req2_ref[me]
    w1s[...] = w1s_ref[...].T
    w1n[...] = w1n_ref[...].T
    classes, half = w2s_ref.shape[0], w2.shape[0] // 2
    w2[...] = jnp.zeros_like(w2)
    w2[:classes] = w2s_ref[...]
    w2[half : half + classes] = w2n_ref[...]
    bias1 = jnp.broadcast_to(bias1_ref[...], (8, bias1_ref.shape[1])).T[:, :1]
    load.wait()

    step = 4 * LANES if rows.shape[0] % (4 * LANES) == 0 else LANES

    def transpose(i, carry):
        rows[tile(i, step), :] = table[:, tile(i, step)].T.astype(jnp.float32)
        return carry

    lax.fori_loop(0, rows.shape[0] // step, transpose, 0)
    wait_all(0, req_ref, asked)
    wait_all(1, req2_ref, asked2)
    to_scalars = pltpu.make_async_copy(asked, ids, local_sem)
    to_scalars.start()
    to_scalars.wait()

    def pick(asker):
        for j in range(cap):
            block[j : j + 1, :] = rows[pl.ds(ids[asker, 0, j], 1), :]
        return block[...].T.astype(jnp.bfloat16)

    got[me] = pick(me)
    send[partner(1)] = pick(partner(1))

    def pick_and_send(t, carry):
        send[partner(t)] = pick(partner(t))
        copy(2, send, got, partner(t - 1)).start()
        return carry

    lax.fori_loop(2, devices, pick_and_send, 0)
    onehot_slots(asked2, onehot)
    copy(2, send, got, partner(devices - 1)).start()
    count_slots(front_ref, own, near, cap, early, devices)
    wait_all(2, send, got)

    lay_side_by_side(count1_ref, got, flat)
    wide = 2 * LANES
    fan_two, fan_one = float(front_ref.shape[0] - 1), float(seed_ref.shape[0] - 1)

    def nodes_chunk(c, carry):
        cols = tile(c, wide)
        mine = dot32(flat[...], own[:, cols]).astype(jnp.bfloat16)
        summed = (dot32(flat[...], near[:, cols]) / fan_two).astype(jnp.bfloat16)
        preact = dot32(w1s[...], mine) + dot32(w1n[...], summed) + bias1
        hidden = jnp.maximum(preact, 0.0).astype(jnp.bfloat16)
        payload[:, cols] = dot32(w2[...], hidden).astype(jnp.bfloat16)
        return carry

    lax.fori_loop(0, own.shape[1] // wide, nodes_chunk, 0)
    cap_two = req2_ref.shape[2]

    def chosen(asker):
        return dot32(payload[...], onehot[:, tile(asker, cap_two)]).astype(jnp.bfloat16)

    got2[me] = chosen(me)
    send2[partner(1)] = chosen(partner(1))

    def choose_and_send(t, carry):
        send2[partner(t)] = chosen(partner(t))
        copy(3, send2, got2, partner(t - 1)).start()
        return carry

    lax.fori_loop(2, devices, choose_and_send, 0)
    copy(3, send2, got2, partner(devices - 1)).start()
    count_slots(seed_ref, seed_own, seed_near, cap_two, 0, devices)
    wait_all(3, send2, got2)
    lay_side_by_side(count2_ref, got2, flat2)
    self_term = dot32(flat2[:half], seed_own[...])
    near_term = dot32(flat2[half:], seed_near[...]) / fan_one
    out_ref[...] = (self_term + near_term)[:classes]


def mask_rows(received, counts, capacity):
    is_live = (jnp.arange(capacity, dtype=jnp.int32)[None, :] < counts[:, None]).reshape(-1)
    flat = received.reshape(-1, received.shape[-1])
    return jnp.where(is_live[:, None], flat, jnp.zeros((), flat.dtype))


def right_product(rows, weight):
    return lax.dot_general(
        rows, weight, (((1,), (1,)), ((), ())), preferred_element_type=jnp.float32
    )


def take_body(
    table_t,
    req_rows,
    count1,
    frontier_list,
    req2_rows,
    count2,
    seed_list,
    w1_self,
    w1_neigh,
    bias1,
    w2_self,
    w2_neigh,
    bias2,
):
    feat_width = table_t.shape[0]
    capacity = req_rows.shape[1]
    table_rows = table_t.T
    picked_rows = jnp.take(
        table_rows,
        lax.all_to_all(req_rows, AXES, split_axis=0, concat_axis=0, tiled=True),
        axis=0,
    )
    received = lax.all_to_all(
        picked_rows, AXES, split_axis=0, concat_axis=0, tiled=True
    )
    flat = mask_rows(received, count1, capacity)
    fanout_two = frontier_list.shape[0] - 1
    front_nodes = frontier_list.shape[1]
    picked = jnp.take(flat, frontier_list.reshape(-1), axis=0).reshape(
        fanout_two + 1, front_nodes, feat_width
    )
    summed = (jnp.sum(picked[1:].astype(jnp.float32), axis=0) / fanout_two).astype(jnp.bfloat16)
    preact = right_product(picked[0], w1_self) + right_product(summed, w1_neigh) + bias1[None, :]
    hidden_rows = jax.nn.relu(preact).astype(jnp.bfloat16)
    cap_two = req2_rows.shape[1]
    payload = jnp.concatenate(
        [right_product(hidden_rows, w2_self), right_product(hidden_rows, w2_neigh)], axis=1
    )
    chosen = jnp.take(
        payload,
        lax.all_to_all(req2_rows, AXES, split_axis=0, concat_axis=0, tiled=True),
        axis=0,
    )
    got_back = lax.all_to_all(chosen, AXES, split_axis=0, concat_axis=0, tiled=True)
    flat_two = mask_rows(got_back, count2, cap_two)
    fanout_one = seed_list.shape[0] - 1
    seed_nodes = seed_list.shape[1]
    picked_two = jnp.take(flat_two, seed_list.reshape(-1), axis=0).reshape(
        fanout_one + 1, seed_nodes, flat_two.shape[1]
    )
    classes = w2_self.shape[0]
    near = jnp.sum(picked_two[1:, :, classes:], axis=0) / fanout_one
    logits = (picked_two[0, :, :classes] + near).T + bias2[:, None]
    return logits


def body(
    table_t,
    req_rows,
    count1,
    frontier_list,
    req2_rows,
    count2,
    seed_list,
    w1_self,
    w1_neigh,
    bias1,
    w2_self,
    w2_neigh,
    bias2,
):
    devices, cap = req_rows.shape
    cap_two = req2_rows.shape[1]
    nodes = frontier_list.shape[1]
    if devices * max(cap, cap_two) * nodes > MATRIX_LIMIT:
        return take_body(
            table_t,
            req_rows,
            count1,
            frontier_list,
            req2_rows,
            count2,
            seed_list,
            w1_self,
            w1_neigh,
            bias1,
            w2_self,
            w2_neigh,
            bias2,
        )
    width, table_rows = table_t.shape
    seeds = seed_list.shape[1]
    hidden_width, classes = w1_self.shape[0], w2_self.shape[0]
    rows_two = 2 * (-(-classes // 16) * 16)
    slots, slots_two = devices * cap, devices * cap_two
    bf16, f32, i32 = jnp.bfloat16, jnp.float32, jnp.int32
    logits = pl.pallas_call(
        functools.partial(whole_kernel, lax.axis_size(AXES[1])),
        in_specs=[pl.BlockSpec(memory_space=pl.ANY)] + [VMEM_ALL] * 2 + [SMEM_ALL] * 2 + [VMEM_ALL] * 7,
        out_specs=VMEM_ALL,
        out_shape=jax.ShapeDtypeStruct((classes, seeds), f32),
        scratch_shapes=[
            pltpu.VMEM((width, table_rows), bf16),
            pltpu.VMEM((hidden_width, width), bf16),
            pltpu.VMEM((hidden_width, width), bf16),
            pltpu.VMEM((rows_two, hidden_width), bf16),
            pltpu.VMEM((devices, 1, cap), i32),
            pltpu.VMEM((devices, 1, cap_two), i32),
            pltpu.SMEM((devices, 1, cap), i32),
            pltpu.VMEM((table_rows, width), f32),
            pltpu.VMEM((cap, width), f32),
            pltpu.VMEM((devices, width, cap), bf16),
            pltpu.VMEM((devices, width, cap), bf16),
            pltpu.VMEM((slots, nodes), bf16),
            pltpu.VMEM((slots, nodes), bf16),
            pltpu.VMEM((nodes, slots_two), bf16),
            pltpu.VMEM((slots_two, seeds), bf16),
            pltpu.VMEM((slots_two, seeds), bf16),
            pltpu.VMEM((width, slots), bf16),
            pltpu.VMEM((rows_two, nodes), bf16),
            pltpu.VMEM((devices, rows_two, cap_two), bf16),
            pltpu.VMEM((devices, rows_two, cap_two), bf16),
            pltpu.VMEM((rows_two, slots_two), bf16),
            pltpu.SemaphoreType.DMA,
            pltpu.SemaphoreType.DMA,
            pltpu.SemaphoreType.DMA((8, devices)),
        ],
        compiler_params=pltpu.CompilerParams(
            vmem_limit_bytes=63 * MIB, collective_id=0, has_side_effects=True
        ),
    )(
        table_t,
        req_rows[:, None, :],
        req2_rows[:, None, :],
        count1,
        count2,
        frontier_list,
        seed_list,
        w1_self.T,
        w1_neigh.T,
        bias1[None, :],
        w2_self,
        w2_neigh,
    )
    return logits + bias2[:, None]


def solution(mesh):
    in_specs = (
        P(None, AXES),
        P(AXES, None),
        P(AXES),
        P(None, AXES),
        P(AXES, None),
        P(AXES),
        P(None, AXES),
        P(),
        P(),
        P(),
        P(),
        P(),
        P(),
    )
    return jax.shard_map(
        body, mesh=mesh, in_specs=in_specs, out_specs=P(None, AXES), check_vma=False
    )
```

profile of v0, /device:TPU:15, one launch (start us, length us, event | category | flops | bytes accessed | tf_op | source)
XLA Modules:
  0.0 65.4 jit_solution(13002325038335293542)
XLA Ops:
  0.0 0.0 copy-start
  0.0 63.8 %shard_map.127 = f32[47,256]{1,0:T(8,128)} custom-call(bf16[100,19456]{1,0:T(8,128)(2,1)} %table_ref.1, s32[32,1,128]{2,1,0:T(1,128)} %bitcast.7, s32[32,1,128]{2,1,0:T(1,128)} %bitcast.8, s32[32]{0:T(128)} %count1_ref.1, s32[32]{0:T(128)} %count2_ref.1, s32[11,1024]{1,0:T(8,128)} %front_ref.1, s32[16,256]{1,0:T(8,128)} %seed_ref.1, ...), custom_call_target="tpu_custom_call" | custom-call | tf_op jit(solution)/shard_map/pallas_call | solution.py:373
  63.8 0.0 copy-done
  63.9 1.5 %broadcast_add_fusion = f32[47,256]{1,0:T(8,128)} fusion(f32[47,256]{1,0:T(8,128)} %shard_map.127, f32[47]{0:T(128)S(1)} %copy-done), kind=kLoop, calls=%fused_computation | loop fusion | flops 12032 | bytes 96444 | tf_op jit(solution)/shard_map/add | solution.py:421
Async XLA Ops:
  0.0 63.8 %copy-start = (f32[47]{0:T(128)S(1)}, f32[47]{0:T(128)}, u32[]{:S(2)}) copy-start(f32[47]{0:T(128)} %param.25) | copy-start | bytes 568
where the time goes:
time: 65.6 us; the launch traced here: 65.4 us
  Pallas kernels  63.8 us (97%)
  other arithmetic  1.49 us (2%)
    pallas_call x1, Pallas kernels, body(): pl.pallas_call(functools.partial(whole_kernel, lax.axis_size(AXES[1])), i...  63.8 us
    add x1, other arithmetic, body(): return logits + bias2[:, None]  1.49 us

commit v1 on v0

v1 whole, which is shorter than its diff:
```python
import functools

import jax
import jax.numpy as jnp
from jax import lax
from jax.experimental import pallas as pl
from jax.experimental.pallas import tpu as pltpu
from jax.sharding import PartitionSpec as P

AXES = ("shard", "grp")
LANES = 128
MIB = 1024 * 1024
MATRIX_LIMIT = 4 * MIB
EARLY = 5
GROUPS = (0, 16, 24, 30, 32)
LAG = 4


FIELDS = 8
FIELD_BITS = 4


def tile(i, size=LANES):
    return pl.ds(pl.multiple_of(i * size, size), size)


def dot32(a, b):
    return jnp.dot(a, b, preferred_element_type=jnp.float32)


def tile_names(span):
    first = lax.broadcasted_iota(jnp.int32, (16, LANES), 0).astype(jnp.float32)
    return [(first + float(16 * b)).astype(jnp.bfloat16) for b in range(span // 16)]


def hits(row, names):
    few = jnp.broadcast_to(row, (16, row.shape[1])).astype(jnp.bfloat16)
    one, zero = jnp.ones((), jnp.bfloat16), jnp.zeros((), jnp.bfloat16)
    return [jnp.where(few == name, one, zero) for name in names]


def prepare_list(list_ref, key_ref, unit_ref, first_ref, cap):
    words = cap // FIELDS
    entry = list_ref[...]
    owner, slot = entry >> (cap.bit_length() - 1), entry & (cap - 1)
    key_ref[...] = owner * words + (slot & (words - 1))
    unit_ref[...] = jnp.ones((), jnp.int32) << (FIELD_BITS * (slot >> (words.bit_length() - 1)))
    first_ref[...] = entry[0:1].astype(jnp.float32)


def count_tile(key_ref, unit_ref, first, name, names, own_ref, near_ref, own_at, near_at, cols):
    words = name.shape[0]
    total = jnp.zeros(name.shape, jnp.int32)
    for k in range(1, key_ref.shape[0]):
        total = total + jnp.where(key_ref[k : k + 1, cols] == name, unit_ref[k : k + 1, cols], 0)
    for b in range(FIELDS):
        field = (total >> (FIELD_BITS * b)) & (2**FIELD_BITS - 1)
        near_ref[pl.ds(pl.multiple_of(near_at + b * words, words), words), cols] = field.astype(
            jnp.float32
        ).astype(jnp.bfloat16)
    for b, part in enumerate(hits(first, names)):
        own_ref[pl.ds(pl.multiple_of(own_at + b * 16, 16), 16), cols] = part


def count_slots(key_ref, unit_ref, first_ref, own_ref, near_ref, cap, owner_of, first, last):
    across = key_ref.shape[1] // LANES
    some = 4 if across % 4 == 0 else 1
    words = cap // FIELDS
    names = tile_names(cap)
    low = lax.broadcasted_iota(jnp.int32, (words, LANES), 0)

    def one(i, carry):
        at, base = lax.div(i, across // some), lax.rem(i, across // some) * some
        owner = owner_of(at)
        name, start = low + owner * words, (owner * cap).astype(jnp.float32)
        for c in range(some):
            cols = tile(base + c)
            own = first_ref[0:1, cols] - start
            count_tile(
                key_ref, unit_ref, own, name, names, own_ref, near_ref, at * cap, at * cap, cols
            )
        return carry

    lax.fori_loop(first * (across // some), last * (across // some), one, 0)


def select_seeds(lists_ref, key_ref, unit_ref, first_ref, out_ref, me, cap, first, last):
    seeds = lists_ref.shape[3]
    words = cap // FIELDS
    names = tile_names(cap)
    low = lax.broadcasted_iota(jnp.int32, (words, LANES), 0)

    def one(t, carry):
        local = lists_ref[lax.rem(t, 2), lax.div(t, 2)].astype(jnp.int32) - me * cap
        field = local >> (words.bit_length() - 1)
        here = jnp.logical_and(field >= 0, field < FIELDS)
        key_ref[...] = local & (words - 1)
        unit_ref[...] = jnp.where(here, jnp.ones((), jnp.int32) << (FIELD_BITS * (field & (FIELDS - 1))), 0)
        first_ref[...] = local[0:1].astype(jnp.float32)
        for c in range(seeds // LANES):
            cols = slice(c * LANES, (c + 1) * LANES)
            at = t * 2 * cap
            count_tile(
                key_ref, unit_ref, first_ref[0:1, cols], low, names, out_ref, out_ref, at, at + cap, cols
            )
        return carry

    lax.fori_loop(first, last, one, 0)


def onehot_slots(asked_ref, out_ref, cap, first, last):
    nodes = out_ref.shape[0]
    names = tile_names(LANES)

    def one(t, carry):
        wanted = asked_ref[t, 1:2].astype(jnp.float32)
        for b in range(nodes // LANES):
            for c, part in enumerate(hits(wanted - float(b * LANES), names)):
                out_ref[b * LANES + 16 * c : b * LANES + 16 * c + 16, tile(t, cap)] = part
        return carry

    lax.fori_loop(first, last, one, 0)


def whole_kernel(grp, rows_two, *refs):
    req_hbm, req2_hbm, front_hbm, seed_hbm, w1s_hbm, w2s_hbm = (refs[k] for k in (1, 2, 5, 6, 7, 10))
    devices, cap, cap_two = req_hbm.shape[0], req_hbm.shape[2], req2_hbm.shape[2]
    nodes, seeds = front_hbm.shape[1], seed_hbm.shape[1]
    width, hidden_width = w1s_hbm.shape
    wide = -(-width // LANES) * LANES
    bf16 = jnp.bfloat16
    pl.run_scoped(
        functools.partial(inner_kernel, grp, *refs),
        pltpu.VMEM((hidden_width, 2 * wide), bf16),
        pltpu.VMEM((rows_two, hidden_width), bf16),
        pltpu.VMEM((devices * cap, nodes), bf16),
        pltpu.VMEM((devices * cap, nodes), bf16),
        pltpu.VMEM((nodes, devices * cap_two), bf16),
        pltpu.VMEM((2 * devices * cap_two, seeds), bf16),
        pltpu.VMEM((-(-width // 16) * 16, devices * cap), bf16),
        pltpu.VMEM((2 * wide, nodes), bf16),
        pltpu.VMEM((rows_two, nodes), bf16),
        pltpu.VMEM((2, 2, rows_two // 2, 2 * cap_two), bf16),
    )


def inner_kernel(
    grp,
    table_hbm,
    req_hbm,
    req2_hbm,
    count1_hbm,
    count2_hbm,
    front_hbm,
    seed_hbm,
    w1s_hbm,
    w1n_hbm,
    bias1_hbm,
    w2s_hbm,
    w2n_hbm,
    out_ref,
    table,
    req_ref,
    req2_ref,
    count1_ref,
    count2_ref,
    front_ref,
    seed_ref,
    w1s_ref,
    w1n_ref,
    bias1_ref,
    w2s_ref,
    w2n_ref,
    key1,
    unit1,
    first1,
    key2,
    unit2,
    first2,
    ask_out,
    asked,
    ids,
    rows,
    block,
    send,
    got,
    list_out,
    lists,
    acc,
    term_out,
    term_in,
    term,
    send2,
    got2,
    load_sems,
    ids_sem,
    out_sems,
    in_sems,
    group_sems,
    cross_sems,
    w1,
    w2,
    own,
    near,
    onehot,
    select,
    flat,
    pair,
    payload,
    chosen,
):
    devices, _, cap = req_ref.shape
    cap_two = req2_ref.shape[2]
    me = lax.axis_index(AXES[0]) * grp + lax.axis_index(AXES[1])
    half = devices // 2
    bits = devices.bit_length() - 1

    def peer(t):
        total = 0
        for i in range(bits):
            mine = lax.rem(lax.div(me, 2**i), 2)
            if isinstance(t, int):
                bit = 1 - mine if (t >> i) & 1 else mine
            else:
                other = lax.rem(lax.div(t, 2**i), 2)
                bit = mine + other - 2 * mine * other
            total = total + bit * 2**i
        return total

    def step_of(p):
        return half * (1 - lax.rem(p, 2)) + lax.div(p, 2)

    def coordinates(to):
        return (lax.div(to, grp), lax.rem(to, grp))

    def place(t):
        return coordinates(peer(t))

    def remote(src, dst, out_sem, in_sem, to):
        return pltpu.make_async_remote_copy(
            src_ref=src,
            dst_ref=dst,
            send_sem=out_sem,
            recv_sem=in_sem,
            device_id=coordinates(to),
            device_id_type=pl.DeviceIdType.MESH,
        )

    steps = [devices * k // 32 for k in GROUPS]

    def group_of(p):
        return sum((p >= edge) * 1 if isinstance(p, int) else (p >= edge).astype(jnp.int32) for edge in steps[1:-1])

    def feature(to, t, p):
        return remote(send.at[t], got.at[p], out_sems.at[1], group_sems.at[group_of(p)], to)

    def arrived(first, last):
        count = last - first - (first <= 1 < last)
        remote(
            send.at[pl.ds(0, count)],
            got.at[pl.ds(0, count)],
            out_sems.at[1],
            group_sems.at[group_of(first)],
            peer(1),
        ).wait_recv()

    pairs = (
        (front_hbm, front_ref),
        (req_hbm, req_ref),
        (req2_hbm, req2_ref),
        (table_hbm, table),
        (w1s_hbm, w1s_ref),
        (w1n_hbm, w1n_ref),
        (bias1_hbm, bias1_ref),
        (w2s_hbm, w2s_ref),
        (w2n_hbm, w2n_ref),
        (seed_hbm, seed_ref),
        (count1_hbm, count1_ref),
        (count2_hbm, count2_ref),
    )
    loads = [pltpu.make_async_copy(a, b, load_sems.at[i]) for i, (a, b) in enumerate(pairs)]
    for load in loads[:4]:
        load.start()
    barrier = pltpu.get_barrier_semaphore()
    for t in range(devices - 1, 0, -1):
        pl.semaphore_signal(
            barrier, inc=1, device_id=place(t), device_id_type=pl.DeviceIdType.MESH
        )
    for load in loads[4:]:
        load.start()
    loads[0].wait()
    prepare_list(front_ref, key1, unit1, first1, cap)
    loads[1].wait()
    loads[2].wait()
    ask_out[:, 0:1, :] = req_ref[...]
    ask_out[:, 1:2, :] = req2_ref[...]
    early = devices * EARLY // 32

    def owner_at(p):
        return peer(step_of(p))

    count_slots(key1, unit1, first1, own, near, cap, owner_at, 0, early)
    pl.semaphore_wait(barrier, devices - 1)

    couples = devices // 2

    def ask(t):
        return remote(ask_out.at[peer(t)], asked.at[t], out_sems.at[0], in_sems.at[0], peer(t))

    def give(i):
        return remote(list_out, lists.at[0, i], out_sems.at[2], in_sems.at[1], peer(2 * i))

    def hand_on():
        return remote(lists.at[0], lists.at[1], out_sems.at[3], in_sems.at[2], peer(1))

    for t in range(devices - 1, 0, -1):
        ask(t).start()
    asked[0] = ask_out[me]
    for load in loads[3:9]:
        load.wait()
    width, hidden_width = w1s_ref.shape[0], w1.shape[0]
    wide = w1.shape[1] // 2
    classes, half_rows = w2s_ref.shape[0], w2.shape[0] // 2
    w1[...] = jnp.zeros_like(w1)
    w1[:, :width] = w1s_ref[...].T
    w1[:, wide : wide + width] = w1n_ref[...].T
    w2[...] = jnp.zeros_like(w2)
    w2[:classes] = w2s_ref[...]
    w2[half_rows : half_rows + classes] = w2n_ref[...]
    pair[...] = jnp.zeros_like(pair)
    bias1 = jnp.broadcast_to(bias1_ref[...], (8, hidden_width)).T[:, :1]

    step = 4 * LANES if rows.shape[0] % (4 * LANES) == 0 else LANES

    def transpose(i, carry):
        rows[tile(i, step), :] = table[:, tile(i, step)].T.astype(jnp.float32)
        return carry

    pieces = rows.shape[0] // step
    lax.fori_loop(0, pieces // 2, transpose, 0)
    for load in loads[9:]:
        load.wait()
    entry = seed_ref[...]
    owner, slot = entry >> (cap_two.bit_length() - 1), entry & (cap_two - 1)

    def limit_of(o, limit):
        return jnp.where(owner == o, count2_ref[o], limit)

    live = slot < lax.fori_loop(0, devices, limit_of, jnp.zeros_like(entry))
    list_out[...] = jnp.where(live, entry, -1).astype(list_out.dtype)
    lists[0, 0] = list_out[...]
    for i in range(couples - 1, 0, -1):
        give(i).start()
    lax.fori_loop(pieces // 2, pieces * 3 // 4, transpose, 0)
    remote(ask_out.at[pl.ds(0, devices - 1)], asked.at[pl.ds(1, devices - 1)], out_sems.at[0], in_sems.at[0], peer(1)).wait()
    to_scalars = pltpu.make_async_copy(asked, ids, ids_sem)
    to_scalars.start()
    lax.fori_loop(pieces * 3 // 4, pieces, transpose, 0)
    to_scalars.wait()

    def pick(t, at):
        for j in range(cap):
            block[at, j : j + 1, :] = rows[pl.ds(ids[t, 0, j], 1), :]
        return block[at].T.astype(jnp.bfloat16)

    def pick_and_send(i, carry):
        to, before = peer(i), peer(i - 1)
        send[half + i] = pick(half + i, 0)
        send[i] = pick(i, 1)
        feature(lax.rem(before + half, devices), half + i - 1, 2 * i - 2).start()
        feature(before, i - 1, 2 * i - 1).start()
        return carry

    send[half] = pick(half, 0)
    got[1] = pick(0, 1)
    send[half + 1] = pick(half + 1, 0)
    feature(peer(half), half, 0).start()
    send[1] = pick(1, 1)
    lax.fori_loop(2, half, pick_and_send, 0)
    onehot_slots(asked, onehot, cap_two, 0, 2)
    feature(peer(devices - 1), devices - 1, devices - 2).start()
    feature(peer(half - 1), half - 1, devices - 1).start()
    onehot_slots(asked, onehot, cap_two, 2, devices)
    remote(lists.at[0, pl.ds(0, couples - 1)], lists.at[0, pl.ds(1, couples - 1)], out_sems.at[2], in_sems.at[1], peer(1)).wait()
    hand_on().start()
    count_slots(key1, unit1, first1, own, near, cap, owner_at, early, devices)
    hand_on().wait()
    select_seeds(lists, key2, unit2, first2, select, me, cap_two, 0, devices)
    nodes = own.shape[1]
    chunk = 2 * LANES
    def lay(p, carry):
        slot = lax.broadcasted_iota(jnp.int32, got.shape[1:], 1)
        live = jnp.where(slot < count1_ref[owner_at(p)], got[p].astype(jnp.float32), 0.0)
        flat[:width, tile(p, cap)] = live.astype(jnp.bfloat16)
        return carry

    def arrive(first, last):
        arrived(first, last)
        lax.fori_loop(first, last, lay, 0)

    arrive(0, steps[1])

    def add_up(first, last, fresh):
        for c in range(nodes // chunk):
            cols = slice(c * chunk, (c + 1) * chunk)
            for m, matrix in enumerate((own, near)):
                part = dot32(flat[:width, first * cap : last * cap], matrix[first * cap : last * cap, cols])
                acc[m, :, cols] = part if fresh else acc[m, :, cols] + part

    add_up(0, steps[1], True)
    for first, last in zip(steps[1:-2], steps[2:-1]):
        arrive(first, last)
        add_up(first, last, False)
    fan_two, fan_one = 1.0 / (front_ref.shape[0] - 1), 1.0 / (seed_ref.shape[0] - 1)
    arrive(steps[-2], steps[-1])
    tail = slice(steps[-2] * cap, steps[-1] * cap)
    scale = jnp.where(lax.broadcasted_iota(jnp.int32, (w2.shape[0], 1), 0) < half_rows, 1.0, fan_one)
    for c in range(nodes // chunk):
        cols = slice(c * chunk, (c + 1) * chunk)
        mine = acc[0, :, cols] + dot32(flat[:width, tail], own[tail, cols])
        summed = (acc[1, :, cols] + dot32(flat[:width, tail], near[tail, cols])) * fan_two
        pair[:width, cols] = mine.astype(jnp.bfloat16)
        pair[wide : wide + width, cols] = summed.astype(jnp.bfloat16)
    for c in range(nodes // chunk):
        cols = slice(c * chunk, (c + 1) * chunk)
        preact = dot32(w1[...], pair[:, cols]) + bias1
        hidden = jnp.maximum(preact, 0.0).astype(jnp.bfloat16)
        payload[:, cols] = (dot32(w2[...], hidden) * scale).astype(jnp.bfloat16)
    def couple_of(s):
        if isinstance(s, int):
            return 0 if s == couples - 1 else 1 + (s + couples // 2 - 1) % (couples - 1)
        return 1 + lax.rem(s + couples // 2 - 1, couples - 1)

    def choose(i, at):
        both = dot32(payload[...], onehot[:, tile(i, 2 * cap_two)]).astype(jnp.bfloat16)
        for c in range(2):
            cols = slice(c * cap_two, (c + 1) * cap_two)
            chosen[at, c, :, :cap_two] = both[:half_rows, cols]
            chosen[at, c, :, cap_two:] = both[half_rows:, cols]

    def terms(i, at):
        term[i] = dot32(chosen[at, 0], select[tile(2 * i, 2 * cap_two), :])
        term_out[i] = dot32(chosen[at, 1], select[tile(2 * i + 1, 2 * cap_two), :])

    def cross(s):
        i = couple_of(s)
        return remote(term_out.at[i], term_in.at[i], out_sems.at[4], cross_sems.at[i], peer(1))

    def join(s):
        cross(s).wait_recv()
        i = couple_of(s)
        send2[i] = (term[i] + term_in[i]).astype(jnp.bfloat16)

    def away(s):
        i = couple_of(s)
        return remote(send2.at[i], got2.at[i], out_sems.at[5], in_sems.at[3], peer(2 * i))

    def steady(s, carry, far=True):
        at = s % 2 if isinstance(s, int) else lax.rem(s, 2)
        terms(couple_of(s), at)
        if not isinstance(s, int) or s < couples - 1:
            choose(couple_of(s + 1), 1 - at)
        if not isinstance(s, int) or s >= 1:
            cross(s - 1).start()
        if not isinstance(s, int) or s >= LAG:
            join(s - LAG)
        if not isinstance(s, int) or s > LAG:
            away(s - LAG - 1).start()
        return carry

    choose(couple_of(0), 0)
    for s in range(LAG + 1):
        steady(s, 0)
    lax.fori_loop(LAG + 1, couples - 2, steady, 0)
    steady(couples - 2, 0)
    steady(couples - 1, 0)
    cross(couples - 1).start()
    for s in range(couples - LAG, couples):
        if s < couples - 1:
            join(s)
        else:
            cross(s).wait_recv()
        away(s - 1).start()
    total = term[0] + term_in[0]
    for src, dst, k in ((send, got, 1), (term_out, term_in, 4), (send2, got2, 5)):
        sent = src.shape[0] - (k != 4)
        whole = remote(src.at[pl.ds(0, sent)], dst.at[pl.ds(0, sent)], out_sems.at[k], in_sems.at[3], peer(1))
        if k == 5:
            whole.wait()
        else:
            whole.wait_send()
    for i in range(1, couples):
        total = total + got2[i].astype(jnp.float32)
    out_ref[...] = total[:classes]


def mask_rows(received, counts, capacity):
    is_live = (jnp.arange(capacity, dtype=jnp.int32)[None, :] < counts[:, None]).reshape(-1)
    flat = received.reshape(-1, received.shape[-1])
    return jnp.where(is_live[:, None], flat, jnp.zeros((), flat.dtype))


def right_product(rows, weight):
    return lax.dot_general(
        rows, weight, (((1,), (1,)), ((), ())), preferred_element_type=jnp.float32
    )


def take_body(
    table_t,
    req_rows,
    count1,
    frontier_list,
    req2_rows,
    count2,
    seed_list,
    w1_self,
    w1_neigh,
    bias1,
    w2_self,
    w2_neigh,
    bias2,
):
    feat_width = table_t.shape[0]
    capacity = req_rows.shape[1]
    table_rows = table_t.T
    picked_rows = jnp.take(
        table_rows,
        lax.all_to_all(req_rows, AXES, split_axis=0, concat_axis=0, tiled=True),
        axis=0,
    )
    received = lax.all_to_all(
        picked_rows, AXES, split_axis=0, concat_axis=0, tiled=True
    )
    flat = mask_rows(received, count1, capacity)
    fanout_two = frontier_list.shape[0] - 1
    front_nodes = frontier_list.shape[1]
    picked = jnp.take(flat, frontier_list.reshape(-1), axis=0).reshape(
        fanout_two + 1, front_nodes, feat_width
    )
    summed = (jnp.sum(picked[1:].astype(jnp.float32), axis=0) / fanout_two).astype(jnp.bfloat16)
    preact = right_product(picked[0], w1_self) + right_product(summed, w1_neigh) + bias1[None, :]
    hidden_rows = jax.nn.relu(preact).astype(jnp.bfloat16)
    cap_two = req2_rows.shape[1]
    payload = jnp.concatenate(
        [right_product(hidden_rows, w2_self), right_product(hidden_rows, w2_neigh)], axis=1
    )
    chosen = jnp.take(
        payload,
        lax.all_to_all(req2_rows, AXES, split_axis=0, concat_axis=0, tiled=True),
        axis=0,
    )
    got_back = lax.all_to_all(chosen, AXES, split_axis=0, concat_axis=0, tiled=True)
    flat_two = mask_rows(got_back, count2, cap_two)
    fanout_one = seed_list.shape[0] - 1
    seed_nodes = seed_list.shape[1]
    picked_two = jnp.take(flat_two, seed_list.reshape(-1), axis=0).reshape(
        fanout_one + 1, seed_nodes, flat_two.shape[1]
    )
    classes = w2_self.shape[0]
    near = jnp.sum(picked_two[1:, :, classes:], axis=0) / fanout_one
    logits = (picked_two[0, :, :classes] + near).T + bias2[:, None]
    return logits


def body(
    table_t,
    req_rows,
    count1,
    frontier_list,
    req2_rows,
    count2,
    seed_list,
    w1_self,
    w1_neigh,
    bias1,
    w2_self,
    w2_neigh,
    bias2,
):
    devices, cap = req_rows.shape
    cap_two = req2_rows.shape[1]
    nodes = frontier_list.shape[1]
    small = devices * max(cap, cap_two) * nodes <= MATRIX_LIMIT
    even = devices >= 32 and devices & (devices - 1) == 0
    plain = cap == cap_two == LANES and nodes % (2 * LANES) == 0
    few = max(frontier_list.shape[0], seed_list.shape[0]) <= 2**FIELD_BITS
    if not (small and even and plain and few):
        return take_body(
            table_t,
            req_rows,
            count1,
            frontier_list,
            req2_rows,
            count2,
            seed_list,
            w1_self,
            w1_neigh,
            bias1,
            w2_self,
            w2_neigh,
            bias2,
        )
    width, table_rows = table_t.shape
    entries, entries_two = frontier_list.shape[0], seed_list.shape[0]
    seeds = seed_list.shape[1]
    hidden_width, classes = w1_self.shape[0], w2_self.shape[0]
    rows_two = 2 * (-(-classes // 16) * 16)
    bf16, f32, i32 = jnp.bfloat16, jnp.float32, jnp.int32
    logits = pl.pallas_call(
        functools.partial(whole_kernel, lax.axis_size(AXES[1]), rows_two),
        in_specs=[pl.BlockSpec(memory_space=pl.ANY)] * 12,
        out_specs=pl.BlockSpec(memory_space=pltpu.VMEM),
        out_shape=jax.ShapeDtypeStruct((classes, seeds), f32),
        scratch_shapes=[
            pltpu.VMEM((width, table_rows), bf16),
            pltpu.VMEM((devices, 1, cap), i32),
            pltpu.VMEM((devices, 1, cap_two), i32),
            pltpu.SMEM((devices,), i32),
            pltpu.SMEM((devices,), i32),
            pltpu.VMEM((entries, nodes), i32),
            pltpu.VMEM((entries_two, seeds), i32),
            pltpu.VMEM((width, hidden_width), bf16),
            pltpu.VMEM((width, hidden_width), bf16),
            pltpu.VMEM((1, hidden_width), f32),
            pltpu.VMEM((classes, hidden_width), bf16),
            pltpu.VMEM((classes, hidden_width), bf16),
            pltpu.VMEM((entries, nodes), i32),
            pltpu.VMEM((entries, nodes), i32),
            pltpu.VMEM((1, nodes), f32),
            pltpu.VMEM((entries_two, seeds), i32),
            pltpu.VMEM((entries_two, seeds), i32),
            pltpu.VMEM((1, seeds), f32),
            pltpu.VMEM((devices, 2, cap), i32),
            pltpu.VMEM((devices, 2, cap), i32),
            pltpu.SMEM((devices, 2, cap), i32),
            pltpu.VMEM((table_rows, width), f32),
            pltpu.VMEM((2, cap, width), f32),
            pltpu.VMEM((devices, width, cap), bf16),
            pltpu.VMEM((devices, width, cap), bf16),
            pltpu.VMEM((entries_two, seeds), jnp.int16),
            pltpu.VMEM((2, devices // 2, entries_two, seeds), jnp.int16),
            pltpu.VMEM((2, width, nodes), f32),
            pltpu.VMEM((devices // 2, rows_two // 2, seeds), f32),
            pltpu.VMEM((devices // 2, rows_two // 2, seeds), f32),
            pltpu.VMEM((devices // 2, rows_two // 2, seeds), f32),
            pltpu.VMEM((devices // 2, rows_two // 2, seeds), bf16),
            pltpu.VMEM((devices // 2, rows_two // 2, seeds), bf16),
            pltpu.SemaphoreType.DMA((12,)),
            pltpu.SemaphoreType.DMA,
            pltpu.SemaphoreType.DMA((6,)),
            pltpu.SemaphoreType.DMA((4,)),
            pltpu.SemaphoreType.DMA((len(GROUPS) - 1,)),
            pltpu.SemaphoreType.DMA((devices // 2,)),
        ],
        compiler_params=pltpu.CompilerParams(
            vmem_limit_bytes=63 * MIB, collective_id=0, has_side_effects=True
        ),
    )(
        table_t,
        req_rows[:, None, :],
        req2_rows[:, None, :],
        count1,
        count2,
        frontier_list,
        seed_list,
        w1_self.T,
        w1_neigh.T,
        bias1[None, :],
        w2_self,
        w2_neigh,
    )
    return logits + bias2[:, None]


def solution(mesh):
    in_specs = (
        P(None, AXES),
        P(AXES, None),
        P(AXES),
        P(None, AXES),
        P(AXES, None),
        P(AXES),
        P(None, AXES),
        P(),
        P(),
        P(),
        P(),
        P(),
        P(),
    )
    return jax.shard_map(
        body, mesh=mesh, in_specs=in_specs, out_specs=P(None, AXES), check_vma=False
    )
```

time: 65.6 us -> 50.8 us (0.77)
  the two profiles are of different devices: /device:TPU:15 before, /device:TPU:0 now
where the time goes in v1:
time: 50.8 us; the launch traced here: 50.6 us
  Pallas kernels  49.1 us (97%)
  other arithmetic  1.49 us (3%)
    pallas_call x1, Pallas kernels, body(): pl.pallas_call(functools.partial(whole_kernel, lax.axis_size(AXES[1]), ro...  49.1 us
    add x1, other arithmetic, body(): return logits + bias2[:, None]  1.49 us

profile of v1, /device:TPU:0, one launch (start us, length us, event | category | flops | bytes accessed | tf_op | source)
XLA Modules:
  0.0 50.6 jit_solution(14285481368003909281)
XLA Ops:
  0.0 0.0 copy-start
  0.0 49.1 %shard_map.127 = f32[47,256]{1,0:T(8,128)} custom-call(bf16[100,19456]{1,0:T(8,128)(2,1)} %refs_0_.1, s32[32,1,128]{2,1,0:T(1,128)} %bitcast.7, s32[32,1,128]{2,1,0:T(1,128)} %bitcast.8, s32[32]{0:T(128)} %refs_3_.1, s32[32]{0:T(128)} %refs_4_.1, s32[11,1024]{1,0:T(8,128)} %refs_5_.1, s32[16,256]{1,0:T(8,128)} %refs_6_.1, bf16[100,256]{1,0:T(8,128)(2,1)} %bitcast.5, ...), custom_call_target="tpu_custom_call" | custom-call | tf_op jit(solution)/shard_map/pallas_call | solution.py:610
  49.1 0.0 copy-done
  49.1 1.5 %broadcast_add_fusion = f32[47,256]{1,0:T(8,128)} fusion(f32[47,256]{1,0:T(8,128)} %shard_map.127, f32[47]{0:T(128)S(1)} %copy-done), kind=kLoop, calls=%fused_computation | loop fusion | flops 12032 | bytes 96444 | tf_op jit(solution)/shard_map/add | solution.py:673
Async XLA Ops:
  0.0 49.1 %copy-start = (f32[47]{0:T(128)S(1)}, f32[47]{0:T(128)}, u32[]{:S(2)}) copy-start(f32[47]{0:T(128)} %param.25) | copy-start | bytes 568

commit v2 on v1

--- a/solution.py
+++ b/solution.py
@@ -11,9 +11,9 @@
 LANES = 128
 MIB = 1024 * 1024
 MATRIX_LIMIT = 4 * MIB
-EARLY = 5
+EARLY = 2
 GROUPS = (0, 16, 24, 30, 32)
-LAG = 4
+BRIDGE = 2
 
 
 FIELDS = 8
@@ -48,18 +48,18 @@
     first_ref[...] = entry[0:1].astype(jnp.float32)
 
 
-def count_tile(key_ref, unit_ref, first, name, names, own_ref, near_ref, own_at, near_at, cols):
+def count_tile(key_ref, unit_ref, first, name, names, own_ref, near_ref, own_at, near_at, cols, to):
     words = name.shape[0]
     total = jnp.zeros(name.shape, jnp.int32)
     for k in range(1, key_ref.shape[0]):
         total = total + jnp.where(key_ref[k : k + 1, cols] == name, unit_ref[k : k + 1, cols], 0)
     for b in range(FIELDS):
         field = (total >> (FIELD_BITS * b)) & (2**FIELD_BITS - 1)
-        near_ref[pl.ds(pl.multiple_of(near_at + b * words, words), words), cols] = field.astype(
+        near_ref[to, pl.ds(pl.multiple_of(near_at + b * words, words), words), :] = field.astype(
             jnp.float32
         ).astype(jnp.bfloat16)
     for b, part in enumerate(hits(first, names)):
-        own_ref[pl.ds(pl.multiple_of(own_at + b * 16, 16), 16), cols] = part
+        own_ref[to, pl.ds(pl.multiple_of(own_at + b * 16, 16), 16), :] = part
 
 
 def count_slots(key_ref, unit_ref, first_ref, own_ref, near_ref, cap, owner_of, first, last):
@@ -77,7 +77,7 @@
             cols = tile(base + c)
             own = first_ref[0:1, cols] - start
             count_tile(
-                key_ref, unit_ref, own, name, names, own_ref, near_ref, at * cap, at * cap, cols
+                key_ref, unit_ref, own, name, names, own_ref, near_ref, at * cap, at * cap, cols, base + c
             )
         return carry
 
@@ -99,9 +99,9 @@
         first_ref[...] = local[0:1].astype(jnp.float32)
         for c in range(seeds // LANES):
             cols = slice(c * LANES, (c + 1) * LANES)
-            at = t * 2 * cap
+            to = t * (seeds // LANES) + c
             count_tile(
-                key_ref, unit_ref, first_ref[0:1, cols], low, names, out_ref, out_ref, at, at + cap, cols
+                key_ref, unit_ref, first_ref[0:1, cols], low, names, out_ref, out_ref, 0, cap, cols, to
             )
         return carry
 
@@ -109,14 +109,14 @@
 
 
 def onehot_slots(asked_ref, out_ref, cap, first, last):
-    nodes = out_ref.shape[0]
+    nodes = out_ref.shape[1]
     names = tile_names(LANES)
 
     def one(t, carry):
-        wanted = asked_ref[t, 1:2].astype(jnp.float32)
+        wanted = asked_ref[t].astype(jnp.float32)
         for b in range(nodes // LANES):
             for c, part in enumerate(hits(wanted - float(b * LANES), names)):
-                out_ref[b * LANES + 16 * c : b * LANES + 16 * c + 16, tile(t, cap)] = part
+                out_ref[t, b * LANES + 16 * c : b * LANES + 16 * c + 16, :] = part
         return carry
 
     lax.fori_loop(first, last, one, 0)
@@ -133,14 +133,14 @@
         functools.partial(inner_kernel, grp, *refs),
         pltpu.VMEM((hidden_width, 2 * wide), bf16),
         pltpu.VMEM((rows_two, hidden_width), bf16),
-        pltpu.VMEM((devices * cap, nodes), bf16),
-        pltpu.VMEM((devices * cap, nodes), bf16),
-        pltpu.VMEM((nodes, devices * cap_two), bf16),
-        pltpu.VMEM((2 * devices * cap_two, seeds), bf16),
-        pltpu.VMEM((-(-width // 16) * 16, devices * cap), bf16),
-        pltpu.VMEM((2 * wide, nodes), bf16),
-        pltpu.VMEM((rows_two, nodes), bf16),
-        pltpu.VMEM((2, 2, rows_two // 2, 2 * cap_two), bf16),
+        pltpu.VMEM((nodes // LANES, devices * cap, LANES), bf16),
+        pltpu.VMEM((nodes // LANES, devices * cap, LANES), bf16),
+        pltpu.VMEM((devices, nodes, LANES), bf16),
+        pltpu.VMEM((devices * seeds // LANES, 2 * cap_two, LANES), bf16),
+        pltpu.VMEM((devices, -(-width // 16) * 16, cap), bf16),
+        pltpu.VMEM((nodes // LANES, 2 * wide, LANES), bf16),
+        pltpu.VMEM((nodes // LANES, rows_two, LANES), bf16),
+        pltpu.VMEM((devices // 2, 2, rows_two // 2, 2 * cap_two), bf16),
     )
 
 
@@ -177,7 +177,6 @@
     key2,
     unit2,
     first2,
-    ask_out,
     asked,
     ids,
     rows,
@@ -192,12 +191,15 @@
     term,
     send2,
     got2,
+    bridge_out,
+    bridge_in,
     load_sems,
     ids_sem,
     out_sems,
     in_sems,
     group_sems,
     cross_sems,
+    bridge_sems,
     w1,
     w2,
     own,
@@ -292,20 +294,42 @@
     prepare_list(front_ref, key1, unit1, first1, cap)
     loads[1].wait()
     loads[2].wait()
-    ask_out[:, 0:1, :] = req_ref[...]
-    ask_out[:, 1:2, :] = req2_ref[...]
+    for load in loads[9:]:
+        load.wait()
+    entry = seed_ref[...]
+    owner, slot = entry >> (cap_two.bit_length() - 1), entry & (cap_two - 1)
+
+    limit = jnp.zeros_like(entry)
+    for o in range(devices):
+        limit = jnp.where(owner == o, count2_ref[o], limit)
+    live = slot < limit
+    list_out[...] = jnp.where(live, entry, -1).astype(list_out.dtype)
+    lists[0, 0] = list_out[...]
     early = devices * EARLY // 32
 
     def owner_at(p):
         return peer(step_of(p))
 
     count_slots(key1, unit1, first1, own, near, cap, owner_at, 0, early)
+    loads[3].wait()
+    step = 4 * LANES if rows.shape[0] % (4 * LANES) == 0 else LANES
+
+    def transpose(i, carry):
+        rows[tile(i, step), :] = table[:, tile(i, step)].T.astype(jnp.float32)
+        return carry
+
+    pieces = rows.shape[0] // step
+    first_piece, second_piece = pieces // 8, pieces // 2
+    lax.fori_loop(0, first_piece, transpose, 0)
     pl.semaphore_wait(barrier, devices - 1)
 
     couples = devices // 2
 
     def ask(t):
-        return remote(ask_out.at[peer(t)], asked.at[t], out_sems.at[0], in_sems.at[0], peer(t))
+        return remote(req_ref.at[peer(t)], ids.at[t], out_sems.at[0], in_sems.at[0], peer(t))
+
+    def ask_two(t):
+        return remote(req2_ref.at[peer(t)], asked.at[t], out_sems.at[7], in_sems.at[4], peer(t))
 
     def give(i):
         return remote(list_out, lists.at[0, i], out_sems.at[2], in_sems.at[1], peer(2 * i))
@@ -315,8 +339,44 @@
 
     for t in range(devices - 1, 0, -1):
         ask(t).start()
-    asked[0] = ask_out[me]
-    for load in loads[3:9]:
+    own_ids = pltpu.make_async_copy(req_ref.at[me], ids.at[0], ids_sem)
+    own_ids.start()
+    for t in range(devices - 1, 0, -1):
+        ask_two(t).start()
+    asked[0] = req2_ref[me]
+    lax.fori_loop(first_piece, second_piece, transpose, 0)
+    for i in range(couples - 1, 0, -1):
+        give(i).start()
+    lax.fori_loop(second_piece, pieces, transpose, 0)
+    own_ids.wait()
+    rest = pl.ds(1, devices - 1)
+    remote(req_ref.at[rest], ids.at[rest], out_sems.at[0], in_sems.at[0], peer(1)).wait()
+
+    def pick(t, at):
+        for j in range(cap):
+            block[at, j : j + 1, :] = rows[pl.ds(ids[t, 0, j], 1), :]
+        return block[at].T.astype(jnp.bfloat16)
+
+    def pick_and_send(i, carry):
+        to, before = peer(i), peer(i - 1)
+        send[half + i] = pick(half + i, 0)
+        send[i] = pick(i, 1)
+        feature(lax.rem(before + half, devices), half + i - 1, 2 * i - 2).start()
+        feature(before, i - 1, 2 * i - 1).start()
+        return carry
+
+    send[half] = pick(half, 0)
+    send[half + 1] = pick(half + 1, 1)
+    feature(peer(half), half, 0).start()
+    send[1] = pick(1, 0)
+    got[1] = pick(0, 1)
+    lax.fori_loop(2, half, pick_and_send, 0)
+    remote(req2_ref.at[rest], asked.at[rest], out_sems.at[7], in_sems.at[4], peer(1)).wait()
+    onehot_slots(asked, onehot, cap_two, 0, 2)
+    feature(peer(devices - 1), devices - 1, devices - 2).start()
+    feature(peer(half - 1), half - 1, devices - 1).start()
+    onehot_slots(asked, onehot, cap_two, 2, devices)
+    for load in loads[4:9]:
         load.wait()
     width, hidden_width = w1s_ref.shape[0], w1.shape[0]
     wide = w1.shape[1] // 2
@@ -330,68 +390,17 @@
     pair[...] = jnp.zeros_like(pair)
     bias1 = jnp.broadcast_to(bias1_ref[...], (8, hidden_width)).T[:, :1]
 
-    step = 4 * LANES if rows.shape[0] % (4 * LANES) == 0 else LANES
-
-    def transpose(i, carry):
-        rows[tile(i, step), :] = table[:, tile(i, step)].T.astype(jnp.float32)
-        return carry
-
-    pieces = rows.shape[0] // step
-    lax.fori_loop(0, pieces // 2, transpose, 0)
-    for load in loads[9:]:
-        load.wait()
-    entry = seed_ref[...]
-    owner, slot = entry >> (cap_two.bit_length() - 1), entry & (cap_two - 1)
-
-    def limit_of(o, limit):
-        return jnp.where(owner == o, count2_ref[o], limit)
-
-    live = slot < lax.fori_loop(0, devices, limit_of, jnp.zeros_like(entry))
-    list_out[...] = jnp.where(live, entry, -1).astype(list_out.dtype)
-    lists[0, 0] = list_out[...]
-    for i in range(couples - 1, 0, -1):
-        give(i).start()
-    lax.fori_loop(pieces // 2, pieces * 3 // 4, transpose, 0)
-    remote(ask_out.at[pl.ds(0, devices - 1)], asked.at[pl.ds(1, devices - 1)], out_sems.at[0], in_sems.at[0], peer(1)).wait()
-    to_scalars = pltpu.make_async_copy(asked, ids, ids_sem)
-    to_scalars.start()
-    lax.fori_loop(pieces * 3 // 4, pieces, transpose, 0)
-    to_scalars.wait()
-
-    def pick(t, at):
-        for j in range(cap):
-            block[at, j : j + 1, :] = rows[pl.ds(ids[t, 0, j], 1), :]
-        return block[at].T.astype(jnp.bfloat16)
-
-    def pick_and_send(i, carry):
-        to, before = peer(i), peer(i - 1)
-        send[half + i] = pick(half + i, 0)
-        send[i] = pick(i, 1)
-        feature(lax.rem(before + half, devices), half + i - 1, 2 * i - 2).start()
-        feature(before, i - 1, 2 * i - 1).start()
-        return carry
-
-    send[half] = pick(half, 0)
-    got[1] = pick(0, 1)
-    send[half + 1] = pick(half + 1, 0)
-    feature(peer(half), half, 0).start()
-    send[1] = pick(1, 1)
-    lax.fori_loop(2, half, pick_and_send, 0)
-    onehot_slots(asked, onehot, cap_two, 0, 2)
-    feature(peer(devices - 1), devices - 1, devices - 2).start()
-    feature(peer(half - 1), half - 1, devices - 1).start()
-    onehot_slots(asked, onehot, cap_two, 2, devices)
     remote(lists.at[0, pl.ds(0, couples - 1)], lists.at[0, pl.ds(1, couples - 1)], out_sems.at[2], in_sems.at[1], peer(1)).wait()
     hand_on().start()
     count_slots(key1, unit1, first1, own, near, cap, owner_at, early, devices)
     hand_on().wait()
     select_seeds(lists, key2, unit2, first2, select, me, cap_two, 0, devices)
-    nodes = own.shape[1]
+    nodes = own.shape[0] * LANES
     chunk = 2 * LANES
     def lay(p, carry):
         slot = lax.broadcasted_iota(jnp.int32, got.shape[1:], 1)
         live = jnp.where(slot < count1_ref[owner_at(p)], got[p].astype(jnp.float32), 0.0)
-        flat[:width, tile(p, cap)] = live.astype(jnp.bfloat16)
+        flat[p, :width, :] = live.astype(jnp.bfloat16)
         return carry
 
     def arrive(first, last):
@@ -399,12 +408,20 @@
         lax.fori_loop(first, last, lay, 0)
 
     arrive(0, steps[1])
+
+    def side_by_side(parts):
+        return jnp.concatenate(parts, axis=1)
+
+    def picked(matrix, c, first, last):
+        left = side_by_side([flat[p, :width, :] for p in range(first, last)])
+        some = range(c * chunk // LANES, (c + 1) * chunk // LANES)
+        return dot32(left, side_by_side([matrix[n, first * cap : last * cap, :] for n in some]))
 
     def add_up(first, last, fresh):
         for c in range(nodes // chunk):
             cols = slice(c * chunk, (c + 1) * chunk)
             for m, matrix in enumerate((own, near)):
-                part = dot32(flat[:width, first * cap : last * cap], matrix[first * cap : last * cap, cols])
+                part = picked(matrix, c, first, last)
                 acc[m, :, cols] = part if fresh else acc[m, :, cols] + part
 
     add_up(0, steps[1], True)
@@ -413,83 +430,128 @@
         add_up(first, last, False)
     fan_two, fan_one = 1.0 / (front_ref.shape[0] - 1), 1.0 / (seed_ref.shape[0] - 1)
     arrive(steps[-2], steps[-1])
-    tail = slice(steps[-2] * cap, steps[-1] * cap)
     scale = jnp.where(lax.broadcasted_iota(jnp.int32, (w2.shape[0], 1), 0) < half_rows, 1.0, fan_one)
     for c in range(nodes // chunk):
         cols = slice(c * chunk, (c + 1) * chunk)
-        mine = acc[0, :, cols] + dot32(flat[:width, tail], own[tail, cols])
-        summed = (acc[1, :, cols] + dot32(flat[:width, tail], near[tail, cols])) * fan_two
-        pair[:width, cols] = mine.astype(jnp.bfloat16)
-        pair[wide : wide + width, cols] = summed.astype(jnp.bfloat16)
+        mine = acc[0, :, cols] + picked(own, c, steps[-2], steps[-1])
+        summed = (acc[1, :, cols] + picked(near, c, steps[-2], steps[-1])) * fan_two
+        for n in range(chunk // LANES):
+            at, lanes = c * chunk // LANES + n, slice(n * LANES, (n + 1) * LANES)
+            pair[at, :width, :] = mine[:, lanes].astype(jnp.bfloat16)
+            pair[at, wide : wide + width, :] = summed[:, lanes].astype(jnp.bfloat16)
+    hidden = []
     for c in range(nodes // chunk):
-        cols = slice(c * chunk, (c + 1) * chunk)
-        preact = dot32(w1[...], pair[:, cols]) + bias1
-        hidden = jnp.maximum(preact, 0.0).astype(jnp.bfloat16)
-        payload[:, cols] = (dot32(w2[...], hidden) * scale).astype(jnp.bfloat16)
-    def couple_of(s):
-        if isinstance(s, int):
-            return 0 if s == couples - 1 else 1 + (s + couples // 2 - 1) % (couples - 1)
-        return 1 + lax.rem(s + couples // 2 - 1, couples - 1)
-
-    def choose(i, at):
-        both = dot32(payload[...], onehot[:, tile(i, 2 * cap_two)]).astype(jnp.bfloat16)
-        for c in range(2):
-            cols = slice(c * cap_two, (c + 1) * cap_two)
-            chosen[at, c, :, :cap_two] = both[:half_rows, cols]
-            chosen[at, c, :, cap_two:] = both[half_rows:, cols]
-
-    def terms(i, at):
-        term[i] = dot32(chosen[at, 0], select[tile(2 * i, 2 * cap_two), :])
-        term_out[i] = dot32(chosen[at, 1], select[tile(2 * i + 1, 2 * cap_two), :])
-
-    def cross(s):
-        i = couple_of(s)
-        return remote(term_out.at[i], term_in.at[i], out_sems.at[4], cross_sems.at[i], peer(1))
-
-    def join(s):
-        cross(s).wait_recv()
-        i = couple_of(s)
+        some = range(c * chunk // LANES, (c + 1) * chunk // LANES)
+        preact = dot32(w1[...], side_by_side([pair[n] for n in some])) + bias1
+        hidden.append(jnp.maximum(preact, 0.0).astype(jnp.bfloat16))
+    for c in range(nodes // chunk):
+        last = (dot32(w2[...], hidden[c]) * scale).astype(jnp.bfloat16)
+        for n in range(chunk // LANES):
+            payload[c * chunk // LANES + n] = last[:, n * LANES : (n + 1) * LANES]
+    across = term.shape[2] // LANES
+
+    def choose(b):
+        left = side_by_side([payload[n] for n in range(nodes // LANES)])
+        for i in batches[b]:
+            both = dot32(left, side_by_side([onehot[2 * i], onehot[2 * i + 1]])).astype(jnp.bfloat16)
+            for c in range(2):
+                cols = slice(c * cap_two, (c + 1) * cap_two)
+                chosen[i, c, :, :cap_two] = both[:half_rows, cols]
+                chosen[i, c, :, cap_two:] = both[half_rows:, cols]
+
+    def terms(i):
+        for c, out in ((1, term_out), (0, term)):
+            at = (2 * i + c) * across
+            out[i] = dot32(chosen[i, c], side_by_side([select[at + n] for n in range(across)]))
+
+    moved, kept, direct = [], [], []
+    for i in range(couples // 2, couples):
+        (direct if i & 1 else moved if i & BRIDGE else kept).append(i)
+    moved = [i ^ BRIDGE for i in kept]
+    near_ones = list(range(1, couples // 2)) + [0]
+    middle, some = len(near_ones) // 2, len(direct) // 2
+    batches = (direct[:some], moved, direct[some:], kept, near_ones[:middle], near_ones[middle:])
+
+    def prepare(b):
+        for i in batches[b]:
+            terms(i)
+        for i in batches[b]:
+            remote(
+                term_out.at[i], term_in.at[i], out_sems.at[4], cross_sems.at[b], peer(1)
+            ).start()
+
+    def crossed(b):
+        some = pl.ds(0, len(batches[b]))
+        remote(
+            term_out.at[some], term_in.at[some], out_sems.at[4], cross_sems.at[b], peer(1)
+        ).wait_recv()
+
+    def bridge(k):
+        return remote(
+            bridge_out.at[k], bridge_in.at[k], out_sems.at[6], bridge_sems.at[k], peer(2 * BRIDGE)
+        )
+
+    def away(i):
+        return remote(send2.at[i], got2.at[i], out_sems.at[5], in_sems.at[3], peer(2 * i))
+
+    def join(i):
         send2[i] = (term[i] + term_in[i]).astype(jnp.bfloat16)
 
-    def away(s):
-        i = couple_of(s)
-        return remote(send2.at[i], got2.at[i], out_sems.at[5], in_sems.at[3], peer(2 * i))
-
-    def steady(s, carry, far=True):
-        at = s % 2 if isinstance(s, int) else lax.rem(s, 2)
-        terms(couple_of(s), at)
-        if not isinstance(s, int) or s < couples - 1:
-            choose(couple_of(s + 1), 1 - at)
-        if not isinstance(s, int) or s >= 1:
-            cross(s - 1).start()
-        if not isinstance(s, int) or s >= LAG:
-            join(s - LAG)
-        if not isinstance(s, int) or s > LAG:
-            away(s - LAG - 1).start()
-        return carry
-
-    choose(couple_of(0), 0)
-    for s in range(LAG + 1):
-        steady(s, 0)
-    lax.fori_loop(LAG + 1, couples - 2, steady, 0)
-    steady(couples - 2, 0)
-    steady(couples - 1, 0)
-    cross(couples - 1).start()
-    for s in range(couples - LAG, couples):
-        if s < couples - 1:
-            join(s)
-        else:
-            cross(s).wait_recv()
-        away(s - 1).start()
+    def join_and_send(b):
+        for i in batches[b]:
+            if i > 0:
+                join(i)
+        for i in batches[b]:
+            if i > 0:
+                away(i).start()
+
+    choose(0)
+    choose(1)
+    prepare(0)
+    choose(2)
+    prepare(1)
+    prepare(2)
+    crossed(0)
+    join_and_send(0)
+    choose(3)
+    choose(4)
+    crossed(1)
+    for k, i in enumerate(moved):
+        bridge_out[k] = (term[i] + term_in[i]).astype(jnp.bfloat16)
+    for k in range(len(moved)):
+        bridge(k).start()
+    prepare(3)
+    prepare(4)
+    choose(5)
+    crossed(2)
+    join_and_send(2)
+    prepare(5)
+    crossed(3)
+    for i in kept:
+        term[i] = term[i] + term_in[i]
+    crossed(4)
+    join_and_send(4)
+    for k, i in enumerate(kept):
+        bridge(k).wait_recv()
+        send2[i] = (term[i] + bridge_in[k].astype(jnp.float32)).astype(jnp.bfloat16)
+    for i in kept:
+        away(i).start()
+    crossed(5)
+    join_and_send(5)
     total = term[0] + term_in[0]
-    for src, dst, k in ((send, got, 1), (term_out, term_in, 4), (send2, got2, 5)):
-        sent = src.shape[0] - (k != 4)
+    arriving = direct + kept + near_ones[:-1]
+    for src, dst, k, sent in (
+        (send, got, 1, devices - 1),
+        (term_out, term_in, 4, couples),
+        (bridge_out, bridge_in, 6, len(moved)),
+        (send2, got2, 5, len(arriving)),
+    ):
         whole = remote(src.at[pl.ds(0, sent)], dst.at[pl.ds(0, sent)], out_sems.at[k], in_sems.at[3], peer(1))
         if k == 5:
             whole.wait()
         else:
             whole.wait_send()
-    for i in range(1, couples):
+    for i in arriving:
         total = total + got2[i].astype(jnp.float32)
     out_ref[...] = total[:classes]
 
@@ -631,9 +693,8 @@
             pltpu.VMEM((entries_two, seeds), i32),
             pltpu.VMEM((entries_two, seeds), i32),
             pltpu.VMEM((1, seeds), f32),
-            pltpu.VMEM((devices, 2, cap), i32),
-            pltpu.VMEM((devices, 2, cap), i32),
-            pltpu.SMEM((devices, 2, cap), i32),
+            pltpu.VMEM((devices, 1, cap_two), i32),
+            pltpu.SMEM((devices, 1, cap), i32),
             pltpu.VMEM((table_rows, width), f32),
             pltpu.VMEM((2, cap, width), f32),
             pltpu.VMEM((devices, width, cap), bf16),
@@ -646,12 +707,15 @@
             pltpu.VMEM((devices // 2, rows_two // 2, seeds), f32),
             pltpu.VMEM((devices // 2, rows_two // 2, seeds), bf16),
             pltpu.VMEM((devices // 2, rows_two // 2, seeds), bf16),
+            pltpu.VMEM((devices // 16, rows_two // 2, seeds), bf16),
+            pltpu.VMEM((devices // 16, rows_two // 2, seeds), bf16),
             pltpu.SemaphoreType.DMA((12,)),
             pltpu.SemaphoreType.DMA,
+            pltpu.SemaphoreType.DMA((8,)),
+            pltpu.SemaphoreType.DMA((5,)),
+            pltpu.SemaphoreType.DMA((len(GROUPS) - 1,)),
             pltpu.SemaphoreType.DMA((6,)),
-            pltpu.SemaphoreType.DMA((4,)),
-            pltpu.SemaphoreType.DMA((len(GROUPS) - 1,)),
-            pltpu.SemaphoreType.DMA((devices // 2,)),
+            pltpu.SemaphoreType.DMA((devices // 16,)),
         ],
         compiler_params=pltpu.CompilerParams(
             vmem_limit_bytes=63 * MIB, collective_id=0, has_side_effects=True

time: 50.8 us -> 46.8 us (0.921)
  Pallas kernels: 49.1 us -> 45.1 us
    pallas_call x1, Pallas kernels: 49.1 us -> 45.1 us  [body(): pl.pallas_call(functools.partial(whole_kernel, lax.axis_size(AXES[1]), ro...]
where the time goes in v2:
time: 46.8 us; the launch traced here: 46.7 us
  Pallas kernels  45.1 us (96%)
  other arithmetic  1.49 us (3%)
    pallas_call x1, Pallas kernels, body(): pl.pallas_call(functools.partial(whole_kernel, lax.axis_size(AXES[1]), ro...  45.1 us
    add x1, other arithmetic, body(): return logits + bias2[:, None]  1.49 us

profile of v2, /device:TPU:0, one launch (start us, length us, event | category | flops | bytes accessed | tf_op | source)
XLA Modules:
  0.0 46.7 jit_solution(14131230623752778070)
XLA Ops:
  0.0 0.0 copy-start
  0.0 45.1 %shard_map.127 = f32[47,256]{1,0:T(8,128)} custom-call(bf16[100,19456]{1,0:T(8,128)(2,1)} %refs_0_.1, s32[32,1,128]{2,1,0:T(1,128)} %bitcast.7, s32[32,1,128]{2,1,0:T(1,128)} %bitcast.8, s32[32]{0:T(128)} %refs_3_.1, s32[32]{0:T(128)} %refs_4_.1, s32[11,1024]{1,0:T(8,128)} %refs_5_.1, s32[16,256]{1,0:T(8,128)} %refs_6_.1, bf16[100,256]{1,0:T(8,128)(2,1)} %bitcast.5, ...), custom_call_target="tpu_custom_call" | custom-call | tf_op jit(solution)/shard_map/pallas_call | solution.py:672
  45.2 0.0 copy-done
  45.2 1.5 %broadcast_add_fusion = f32[47,256]{1,0:T(8,128)} fusion(f32[47,256]{1,0:T(8,128)} %shard_map.127, f32[47]{0:T(128)S(1)} %copy-done), kind=kLoop, calls=%fused_computation | loop fusion | flops 12032 | bytes 96444 | tf_op jit(solution)/shard_map/add | solution.py:737
Async XLA Ops:
  0.0 45.2 %copy-start = (f32[47]{0:T(128)S(1)}, f32[47]{0:T(128)}, u32[]{:S(2)}) copy-start(f32[47]{0:T(128)} %param.25) | copy-start | bytes 568

commit v3 on v2

--- a/solution.py
+++ b/solution.py
@@ -85,13 +85,19 @@
 
 
 def select_seeds(lists_ref, key_ref, unit_ref, first_ref, out_ref, me, cap, first, last):
-    seeds = lists_ref.shape[3]
+    devices, _, seeds = lists_ref.shape
+    depth = devices // 8
+
+    def step_at(at):
+        core, y = lax.div(at, 4 * depth), lax.rem(lax.div(at, 2 * depth), 2)
+        return core + 2 * y + 4 * lax.rem(lax.div(at, depth), 2) + 8 * lax.rem(at, depth)
+
     words = cap // FIELDS
     names = tile_names(cap)
     low = lax.broadcasted_iota(jnp.int32, (words, LANES), 0)
 
-    def one(t, carry):
-        local = lists_ref[lax.rem(t, 2), lax.div(t, 2)].astype(jnp.int32) - me * cap
+    def one(at, carry):
+        local = lists_ref[at].astype(jnp.int32) - me * cap
         field = local >> (words.bit_length() - 1)
         here = jnp.logical_and(field >= 0, field < FIELDS)
         key_ref[...] = local & (words - 1)
@@ -99,7 +105,7 @@
         first_ref[...] = local[0:1].astype(jnp.float32)
         for c in range(seeds // LANES):
             cols = slice(c * LANES, (c + 1) * LANES)
-            to = t * (seeds // LANES) + c
+            to = step_at(at) * (seeds // LANES) + c
             count_tile(
                 key_ref, unit_ref, first_ref[0:1, cols], low, names, out_ref, out_ref, 0, cap, cols, to
             )
@@ -183,7 +189,8 @@
     block,
     send,
     got,
-    list_out,
+    send_rest,
+    got_rest,
     lists,
     acc,
     term_out,
@@ -200,6 +207,8 @@
     group_sems,
     cross_sems,
     bridge_sems,
+    ask_sems,
+    list_sems,
     w1,
     w2,
     own,
@@ -254,16 +263,21 @@
         return sum((p >= edge) * 1 if isinstance(p, int) else (p >= edge).astype(jnp.int32) for edge in steps[1:-1])
 
     def feature(to, t, p):
-        return remote(send.at[t], got.at[p], out_sems.at[1], group_sems.at[group_of(p)], to)
+        group = group_of(p)
+        remote(send.at[t], got.at[p], out_sems.at[1], group_sems.at[0, group], to).start()
+        remote(
+            send_rest.at[t], got_rest.at[p], out_sems.at[8], group_sems.at[1, group], to
+        ).start()
 
     def arrived(first, last):
         count = last - first - (first <= 1 < last)
+        group = group_of(first)
+        some = pl.ds(0, count)
         remote(
-            send.at[pl.ds(0, count)],
-            got.at[pl.ds(0, count)],
-            out_sems.at[1],
-            group_sems.at[group_of(first)],
-            peer(1),
+            send.at[some], got.at[some], out_sems.at[1], group_sems.at[0, group], peer(1)
+        ).wait_recv()
+        remote(
+            send_rest.at[some], got_rest.at[some], out_sems.at[8], group_sems.at[1, group], peer(1)
         ).wait_recv()
 
     pairs = (
@@ -303,8 +317,7 @@
     for o in range(devices):
         limit = jnp.where(owner == o, count2_ref[o], limit)
     live = slot < limit
-    list_out[...] = jnp.where(live, entry, -1).astype(list_out.dtype)
-    lists[0, 0] = list_out[...]
+    lists[0] = jnp.where(live, entry, -1).astype(lists.dtype)
     early = devices * EARLY // 32
 
     def owner_at(p):
@@ -326,16 +339,38 @@
     couples = devices // 2
 
     def ask(t):
-        return remote(req_ref.at[peer(t)], ids.at[t], out_sems.at[0], in_sems.at[0], peer(t))
+        quarter = t % half // (half // 4)
+        return remote(req_ref.at[peer(t)], ids.at[t], out_sems.at[0], ask_sems.at[quarter], peer(t))
 
     def ask_two(t):
         return remote(req2_ref.at[peer(t)], asked.at[t], out_sems.at[7], in_sems.at[4], peer(t))
 
-    def give(i):
-        return remote(list_out, lists.at[0, i], out_sems.at[2], in_sems.at[1], peer(2 * i))
-
-    def hand_on():
-        return remote(lists.at[0], lists.at[1], out_sems.at[3], in_sems.at[2], peer(1))
+    def hand_on(k):
+        depth = devices // 8
+        if k == 0:
+            return [
+                remote(lists.at[0], lists.at[j], list_sems.at[0, 0], list_sems.at[1, 0], peer(8 * j))
+                for j in range(1, depth)
+            ]
+        count = depth << (k - 1)
+        return [
+            remote(
+                lists.at[pl.ds(0, count)],
+                lists.at[pl.ds(count, count)],
+                list_sems.at[0, k],
+                list_sems.at[1, k],
+                peer(8 >> k),
+            )
+        ]
+
+    def take(k):
+        if k == 0:
+            some = pl.ds(0, devices // 8 - 1)
+            remote(
+                lists.at[some], lists.at[some], list_sems.at[0, 0], list_sems.at[1, 0], peer(1)
+            ).wait()
+        else:
+            hand_on(k)[0].wait()
 
     for t in range(devices - 1, 0, -1):
         ask(t).start()
@@ -344,37 +379,54 @@
     for t in range(devices - 1, 0, -1):
         ask_two(t).start()
     asked[0] = req2_ref[me]
+    for one in hand_on(0):
+        one.start()
     lax.fori_loop(first_piece, second_piece, transpose, 0)
-    for i in range(couples - 1, 0, -1):
-        give(i).start()
     lax.fori_loop(second_piece, pieces, transpose, 0)
     own_ids.wait()
     rest = pl.ds(1, devices - 1)
-    remote(req_ref.at[rest], ids.at[rest], out_sems.at[0], in_sems.at[0], peer(1)).wait()
+
+    def asked_for(count, k):
+        some = pl.ds(0, count)
+        return remote(req_ref.at[some], ids.at[some], out_sems.at[0], ask_sems.at[k], peer(1))
+
+    asked_for(half // 2 - 1, 0).wait_recv()
+
+    main = send.shape[1]
 
     def pick(t, at):
         for j in range(cap):
             block[at, j : j + 1, :] = rows[pl.ds(ids[t, 0, j], 1), :]
-        return block[at].T.astype(jnp.bfloat16)
+        columns = block[at].T.astype(jnp.bfloat16)
+        return columns[:main], columns[main:]
+
+    def put(to, rest, at, columns):
+        to[at], rest[at] = columns
 
     def pick_and_send(i, carry):
         to, before = peer(i), peer(i - 1)
-        send[half + i] = pick(half + i, 0)
-        send[i] = pick(i, 1)
-        feature(lax.rem(before + half, devices), half + i - 1, 2 * i - 2).start()
-        feature(before, i - 1, 2 * i - 1).start()
+        put(send, send_rest, half + i, pick(half + i, 0))
+        put(send, send_rest, i, pick(i, 1))
+        feature(lax.rem(before + half, devices), half + i - 1, 2 * i - 2)
+        feature(before, i - 1, 2 * i - 1)
         return carry
 
-    send[half] = pick(half, 0)
-    send[half + 1] = pick(half + 1, 1)
-    feature(peer(half), half, 0).start()
-    send[1] = pick(1, 0)
-    got[1] = pick(0, 1)
-    lax.fori_loop(2, half, pick_and_send, 0)
+    put(send, send_rest, half, pick(half, 0))
+    put(send, send_rest, half + 1, pick(half + 1, 1))
+    feature(peer(half), half, 0)
+    put(send, send_rest, 1, pick(1, 0))
+    put(got, got_rest, 1, pick(0, 1))
+    lax.fori_loop(2, half // 4, pick_and_send, 0)
+    take(0)
+    hand_on(1)[0].start()
+    for k in range(1, 4):
+        asked_for(half // 2, k).wait_recv()
+        lax.fori_loop(k * half // 4, (k + 1) * half // 4, pick_and_send, 0)
+    asked_for(devices - 1, 0).wait_send()
     remote(req2_ref.at[rest], asked.at[rest], out_sems.at[7], in_sems.at[4], peer(1)).wait()
     onehot_slots(asked, onehot, cap_two, 0, 2)
-    feature(peer(devices - 1), devices - 1, devices - 2).start()
-    feature(peer(half - 1), half - 1, devices - 1).start()
+    feature(peer(devices - 1), devices - 1, devices - 2)
+    feature(peer(half - 1), half - 1, devices - 1)
     onehot_slots(asked, onehot, cap_two, 2, devices)
     for load in loads[4:9]:
         load.wait()
@@ -390,17 +442,22 @@
     pair[...] = jnp.zeros_like(pair)
     bias1 = jnp.broadcast_to(bias1_ref[...], (8, hidden_width)).T[:, :1]
 
-    remote(lists.at[0, pl.ds(0, couples - 1)], lists.at[0, pl.ds(1, couples - 1)], out_sems.at[2], in_sems.at[1], peer(1)).wait()
-    hand_on().start()
-    count_slots(key1, unit1, first1, own, near, cap, owner_at, early, devices)
-    hand_on().wait()
+    take(1)
+    hand_on(2)[0].start()
+    count_slots(key1, unit1, first1, own, near, cap, owner_at, early, devices * 5 // 8)
+    take(2)
+    hand_on(3)[0].start()
+    count_slots(key1, unit1, first1, own, near, cap, owner_at, devices * 5 // 8, devices)
+    take(3)
     select_seeds(lists, key2, unit2, first2, select, me, cap_two, 0, devices)
     nodes = own.shape[0] * LANES
     chunk = 2 * LANES
     def lay(p, carry):
-        slot = lax.broadcasted_iota(jnp.int32, got.shape[1:], 1)
-        live = jnp.where(slot < count1_ref[owner_at(p)], got[p].astype(jnp.float32), 0.0)
-        flat[p, :width, :] = live.astype(jnp.bfloat16)
+        count = count1_ref[owner_at(p)]
+        for part, at, rows_here in ((got, 0, main), (got_rest, main, got_rest.shape[1])):
+            slot = lax.broadcasted_iota(jnp.int32, part.shape[1:], 1)
+            live = jnp.where(slot < count, part[p].astype(jnp.float32), 0.0)
+            flat[p, at : at + rows_here, :] = live.astype(jnp.bfloat16)
         return carry
 
     def arrive(first, last):
@@ -468,9 +525,9 @@
     for i in range(couples // 2, couples):
         (direct if i & 1 else moved if i & BRIDGE else kept).append(i)
     moved = [i ^ BRIDGE for i in kept]
-    near_ones = list(range(1, couples // 2)) + [0]
+    near_ones = [*range(couples // 4, couples // 2), *range(1, couples // 4), 0]
     middle, some = len(near_ones) // 2, len(direct) // 2
-    batches = (direct[:some], moved, direct[some:], kept, near_ones[:middle], near_ones[middle:])
+    batches = (moved, direct[:some], direct[some:], kept, near_ones[:middle], near_ones[middle:])
 
     def prepare(b):
         for i in batches[b]:
@@ -510,38 +567,39 @@
     prepare(0)
     choose(2)
     prepare(1)
-    prepare(2)
     crossed(0)
-    join_and_send(0)
-    choose(3)
-    choose(4)
-    crossed(1)
     for k, i in enumerate(moved):
         bridge_out[k] = (term[i] + term_in[i]).astype(jnp.bfloat16)
     for k in range(len(moved)):
         bridge(k).start()
-    prepare(3)
+    choose(4)
+    prepare(2)
+    crossed(1)
+    join_and_send(1)
+    choose(3)
     prepare(4)
     choose(5)
+    prepare(3)
     crossed(2)
     join_and_send(2)
     prepare(5)
+    crossed(4)
+    join_and_send(4)
     crossed(3)
     for i in kept:
         term[i] = term[i] + term_in[i]
-    crossed(4)
-    join_and_send(4)
+    crossed(5)
+    join_and_send(5)
     for k, i in enumerate(kept):
         bridge(k).wait_recv()
         send2[i] = (term[i] + bridge_in[k].astype(jnp.float32)).astype(jnp.bfloat16)
     for i in kept:
         away(i).start()
-    crossed(5)
-    join_and_send(5)
     total = term[0] + term_in[0]
     arriving = direct + kept + near_ones[:-1]
     for src, dst, k, sent in (
         (send, got, 1, devices - 1),
+        (send_rest, got_rest, 8, devices - 1),
         (term_out, term_in, 4, couples),
         (bridge_out, bridge_in, 6, len(moved)),
         (send2, got2, 5, len(arriving)),
@@ -646,6 +704,7 @@
     small = devices * max(cap, cap_two) * nodes <= MATRIX_LIMIT
     even = devices >= 32 and devices & (devices - 1) == 0
     plain = cap == cap_two == LANES and nodes % (2 * LANES) == 0
+    plain = plain and table_t.shape[0] > 16
     few = max(frontier_list.shape[0], seed_list.shape[0]) <= 2**FIELD_BITS
     if not (small and even and plain and few):
         return take_body(
@@ -669,11 +728,12 @@
     hidden_width, classes = w1_self.shape[0], w2_self.shape[0]
     rows_two = 2 * (-(-classes // 16) * 16)
     bf16, f32, i32 = jnp.bfloat16, jnp.float32, jnp.int32
+    main = (width - 1) // 16 * 16
     logits = pl.pallas_call(
         functools.partial(whole_kernel, lax.axis_size(AXES[1]), rows_two),
         in_specs=[pl.BlockSpec(memory_space=pl.ANY)] * 12,
         out_specs=pl.BlockSpec(memory_space=pltpu.VMEM),
-        out_shape=jax.ShapeDtypeStruct((classes, seeds), f32),
+        out_shape=pltpu.VMEM((classes, seeds), f32),
         scratch_shapes=[
             pltpu.VMEM((width, table_rows), bf16),
             pltpu.VMEM((devices, 1, cap), i32),
@@ -697,10 +757,11 @@
             pltpu.SMEM((devices, 1, cap), i32),
             pltpu.VMEM((table_rows, width), f32),
             pltpu.VMEM((2, cap, width), f32),
-            pltpu.VMEM((devices, width, cap), bf16),
-            pltpu.VMEM((devices, width, cap), bf16),
-            pltpu.VMEM((entries_two, seeds), jnp.int16),
-            pltpu.VMEM((2, devices // 2, entries_two, seeds), jnp.int16),
+            pltpu.VMEM((devices, main, cap), bf16),
+            pltpu.VMEM((devices, main, cap), bf16),
+            pltpu.VMEM((devices, width - main, cap), bf16),
+            pltpu.VMEM((devices, width - main, cap), bf16),
+            pltpu.VMEM((devices, entries_two, seeds), jnp.int16),
             pltpu.VMEM((2, width, nodes), f32),
             pltpu.VMEM((devices // 2, rows_two // 2, seeds), f32),
             pltpu.VMEM((devices // 2, rows_two // 2, seeds), f32),
@@ -711,11 +772,13 @@
             pltpu.VMEM((devices // 16, rows_two // 2, seeds), bf16),
             pltpu.SemaphoreType.DMA((12,)),
             pltpu.SemaphoreType.DMA,
-            pltpu.SemaphoreType.DMA((8,)),
-            pltpu.SemaphoreType.DMA((5,)),
-            pltpu.SemaphoreType.DMA((len(GROUPS) - 1,)),
+            pltpu.SemaphoreType.DMA((9,)),
+            pltpu.SemaphoreType.DMA((6,)),
+            pltpu.SemaphoreType.DMA((2, len(GROUPS) - 1)),
             pltpu.SemaphoreType.DMA((6,)),
             pltpu.SemaphoreType.DMA((devices // 16,)),
+            pltpu.SemaphoreType.DMA((4,)),
+            pltpu.SemaphoreType.DMA((2, 4)),
         ],
         compiler_params=pltpu.CompilerParams(
             vmem_limit_bytes=63 * MIB, collective_id=0, has_side_effects=True

time: 46.8 us -> 43.6 us (0.932)
  Pallas kernels: 45.1 us -> 42.8 us
  other arithmetic: 1.49 us -> 0.7 us
    pallas_call x1, Pallas kernels: 45.1 us -> 42.8 us  [body(): pl.pallas_call(functools.partial(whole_kernel, lax.axis_size(AXES[1]), ro...]
    add x1, other arithmetic: 1.49 us -> 0.7 us  [body(): return logits + bias2[:, None]]
where the time goes in v3:
time: 43.6 us; the launch traced here: 43.5 us
  Pallas kernels  42.8 us (98%)
  other arithmetic  0.7 us (2%)
    pallas_call x1, Pallas kernels, body(): pl.pallas_call(functools.partial(whole_kernel, lax.axis_size(AXES[1]), ro...  42.8 us

profile of v3, /device:TPU:0, one launch (start us, length us, event | category | flops | bytes accessed | tf_op | source)
XLA Modules:
  0.0 43.5 jit_solution(17835443551541011507)
XLA Ops:
  0.0 0.0 copy-start
  0.0 42.8 %shard_map.127 = f32[47,256]{1,0:T(8,128)S(1)} custom-call(bf16[100,19456]{1,0:T(8,128)(2,1)} %refs_0_.1, s32[32,1,128]{2,1,0:T(1,128)} %bitcast.7, s32[32,1,128]{2,1,0:T(1,128)} %bitcast.8, s32[32]{0:T(128)} %refs_3_.1, s32[32]{0:T(128)} %refs_4_.1, s32[11,1024]{1,0:T(8,128)} %refs_5_.1, s32[16,256]{1,0:T(8,128)} %refs_6_.1, bf16[100,256]{1,0:T(8,128)(2,1)} %bitcast.5, ...), custom_call_target="tpu_custom_call" | custom-call | tf_op jit(solution)/shard_map/pallas_call | solution.py:732
  42.8 0.0 copy-done
  42.8 0.7 %broadcast_add_fusion = f32[47,256]{1,0:T(8,128)} fusion(f32[47,256]{1,0:T(8,128)S(1)} %shard_map.127, f32[47]{0:T(128)S(1)} %copy-done), kind=kLoop, calls=%fused_computation | loop fusion | flops 12032 | bytes 96444 | tf_op jit(solution)/shard_map/add | solution.py:800
Async XLA Ops:
  0.0 42.8 %copy-start = (f32[47]{0:T(128)S(1)}, f32[47]{0:T(128)}, u32[]{:S(2)}) copy-start(f32[47]{0:T(128)} %param.25) | copy-start | bytes 568

commit v4 on v3

--- a/solution.py
+++ b/solution.py
@@ -201,8 +201,6 @@
     bridge_out,
     bridge_in,
     load_sems,
-    ids_sem,
-    out_sems,
     in_sems,
     group_sems,
     cross_sems,
@@ -264,9 +262,9 @@
 
     def feature(to, t, p):
         group = group_of(p)
-        remote(send.at[t], got.at[p], out_sems.at[1], group_sems.at[0, group], to).start()
+        remote(send.at[t], got.at[p], load_sems.at[9], group_sems.at[0, group], to).start()
         remote(
-            send_rest.at[t], got_rest.at[p], out_sems.at[8], group_sems.at[1, group], to
+            send_rest.at[t], got_rest.at[p], load_sems.at[10], group_sems.at[1, group], to
         ).start()
 
     def arrived(first, last):
@@ -274,10 +272,10 @@
         group = group_of(first)
         some = pl.ds(0, count)
         remote(
-            send.at[some], got.at[some], out_sems.at[1], group_sems.at[0, group], peer(1)
+            send.at[some], got.at[some], load_sems.at[9], group_sems.at[0, group], peer(1)
         ).wait_recv()
         remote(
-            send_rest.at[some], got_rest.at[some], out_sems.at[8], group_sems.at[1, group], peer(1)
+            send_rest.at[some], got_rest.at[some], load_sems.at[10], group_sems.at[1, group], peer(1)
         ).wait_recv()
 
     pairs = (
@@ -340,16 +338,16 @@
 
     def ask(t):
         quarter = t % half // (half // 4)
-        return remote(req_ref.at[peer(t)], ids.at[t], out_sems.at[0], ask_sems.at[quarter], peer(t))
+        return remote(req_ref.at[peer(t)], ids.at[t], load_sems.at[0], ask_sems.at[quarter], peer(t))
 
     def ask_two(t):
-        return remote(req2_ref.at[peer(t)], asked.at[t], out_sems.at[7], in_sems.at[4], peer(t))
+        return remote(req2_ref.at[peer(t)], asked.at[t], load_sems.at[1], in_sems.at[0], peer(t))
 
     def hand_on(k):
         depth = devices // 8
         if k == 0:
             return [
-                remote(lists.at[0], lists.at[j], list_sems.at[0, 0], list_sems.at[1, 0], peer(8 * j))
+                remote(lists.at[0], lists.at[j], load_sems.at[2], list_sems.at[0], peer(8 * j))
                 for j in range(1, depth)
             ]
         count = depth << (k - 1)
@@ -357,8 +355,8 @@
             remote(
                 lists.at[pl.ds(0, count)],
                 lists.at[pl.ds(count, count)],
-                list_sems.at[0, k],
-                list_sems.at[1, k],
+                load_sems.at[2],
+                list_sems.at[k],
                 peer(8 >> k),
             )
         ]
@@ -367,14 +365,14 @@
         if k == 0:
             some = pl.ds(0, devices // 8 - 1)
             remote(
-                lists.at[some], lists.at[some], list_sems.at[0, 0], list_sems.at[1, 0], peer(1)
+                lists.at[some], lists.at[some], load_sems.at[2], list_sems.at[0], peer(1)
             ).wait()
         else:
             hand_on(k)[0].wait()
 
-    for t in range(devices - 1, 0, -1):
+    for t in sorted(range(1, devices), key=lambda t: (t % half // (half // 4), -t)):
         ask(t).start()
-    own_ids = pltpu.make_async_copy(req_ref.at[me], ids.at[0], ids_sem)
+    own_ids = pltpu.make_async_copy(req_ref.at[me], ids.at[0], load_sems.at[3])
     own_ids.start()
     for t in range(devices - 1, 0, -1):
         ask_two(t).start()
@@ -388,7 +386,7 @@
 
     def asked_for(count, k):
         some = pl.ds(0, count)
-        return remote(req_ref.at[some], ids.at[some], out_sems.at[0], ask_sems.at[k], peer(1))
+        return remote(req_ref.at[some], ids.at[some], load_sems.at[0], ask_sems.at[k], peer(1))
 
     asked_for(half // 2 - 1, 0).wait_recv()
 
@@ -423,7 +421,7 @@
         asked_for(half // 2, k).wait_recv()
         lax.fori_loop(k * half // 4, (k + 1) * half // 4, pick_and_send, 0)
     asked_for(devices - 1, 0).wait_send()
-    remote(req2_ref.at[rest], asked.at[rest], out_sems.at[7], in_sems.at[4], peer(1)).wait()
+    remote(req2_ref.at[rest], asked.at[rest], load_sems.at[1], in_sems.at[0], peer(1)).wait()
     onehot_slots(asked, onehot, cap_two, 0, 2)
     feature(peer(devices - 1), devices - 1, devices - 2)
     feature(peer(half - 1), half - 1, devices - 1)
@@ -534,22 +532,22 @@
             terms(i)
         for i in batches[b]:
             remote(
-                term_out.at[i], term_in.at[i], out_sems.at[4], cross_sems.at[b], peer(1)
+                term_out.at[i], term_in.at[i], load_sems.at[11], cross_sems.at[b], peer(1)
             ).start()
 
     def crossed(b):
         some = pl.ds(0, len(batches[b]))
         remote(
-            term_out.at[some], term_in.at[some], out_sems.at[4], cross_sems.at[b], peer(1)
+            term_out.at[some], term_in.at[some], load_sems.at[11], cross_sems.at[b], peer(1)
         ).wait_recv()
 
     def bridge(k):
         return remote(
-            bridge_out.at[k], bridge_in.at[k], out_sems.at[6], bridge_sems.at[k], peer(2 * BRIDGE)
+            bridge_out.at[k], bridge_in.at[k], load_sems.at[4], bridge_sems.at[k], peer(2 * BRIDGE)
         )
 
     def away(i):
-        return remote(send2.at[i], got2.at[i], out_sems.at[5], in_sems.at[3], peer(2 * i))
+        return remote(send2.at[i], got2.at[i], load_sems.at[5], in_sems.at[1], peer(2 * i))
 
     def join(i):
         send2[i] = (term[i] + term_in[i]).astype(jnp.bfloat16)
@@ -598,13 +596,13 @@
     total = term[0] + term_in[0]
     arriving = direct + kept + near_ones[:-1]
     for src, dst, k, sent in (
-        (send, got, 1, devices - 1),
-        (send_rest, got_rest, 8, devices - 1),
-        (term_out, term_in, 4, couples),
-        (bridge_out, bridge_in, 6, len(moved)),
+        (send, got, 9, devices - 1),
+        (send_rest, got_rest, 10, devices - 1),
+        (term_out, term_in, 11, couples),
+        (bridge_out, bridge_in, 4, len(moved)),
         (send2, got2, 5, len(arriving)),
     ):
-        whole = remote(src.at[pl.ds(0, sent)], dst.at[pl.ds(0, sent)], out_sems.at[k], in_sems.at[3], peer(1))
+        whole = remote(src.at[pl.ds(0, sent)], dst.at[pl.ds(0, sent)], load_sems.at[k], in_sems.at[1], peer(1))
         if k == 5:
             whole.wait()
         else:
@@ -771,14 +769,12 @@
             pltpu.VMEM((devices // 16, rows_two // 2, seeds), bf16),
             pltpu.VMEM((devices // 16, rows_two // 2, seeds), bf16),
             pltpu.SemaphoreType.DMA((12,)),
-            pltpu.SemaphoreType.DMA,
-            pltpu.SemaphoreType.DMA((9,)),
-            pltpu.SemaphoreType.DMA((6,)),
+            pltpu.SemaphoreType.DMA((2,)),
             pltpu.SemaphoreType.DMA((2, len(GROUPS) - 1)),
             pltpu.SemaphoreType.DMA((6,)),
             pltpu.SemaphoreType.DMA((devices // 16,)),
             pltpu.SemaphoreType.DMA((4,)),
-            pltpu.SemaphoreType.DMA((2, 4)),
+            pltpu.SemaphoreType.DMA((4,)),
         ],
         compiler_params=pltpu.CompilerParams(
             vmem_limit_bytes=63 * MIB, collective_id=0, has_side_effects=True

time: 43.6 us -> 43.5 us (level)
  no operation moved by 1% of the time
where the time goes in v4:
time: 43.5 us; the launch traced here: 43.4 us
  Pallas kernels  42.6 us (98%)
  other arithmetic  0.7 us (2%)
    pallas_call x1, Pallas kernels, body(): pl.pallas_call(functools.partial(whole_kernel, lax.axis_size(AXES[1]), ro...  42.6 us

profile of v4, /device:TPU:0, one launch (start us, length us, event | category | flops | bytes accessed | tf_op | source)
XLA Modules:
  0.0 43.4 jit_solution(16430486437808433952)
XLA Ops:
  0.0 0.0 copy-start
  0.0 42.6 %shard_map.127 = f32[47,256]{1,0:T(8,128)S(1)} custom-call(bf16[100,19456]{1,0:T(8,128)(2,1)} %refs_0_.1, s32[32,1,128]{2,1,0:T(1,128)} %bitcast.7, s32[32,1,128]{2,1,0:T(1,128)} %bitcast.8, s32[32]{0:T(128)} %refs_3_.1, s32[32]{0:T(128)} %refs_4_.1, s32[11,1024]{1,0:T(8,128)} %refs_5_.1, s32[16,256]{1,0:T(8,128)} %refs_6_.1, bf16[100,256]{1,0:T(8,128)(2,1)} %bitcast.5, ...), custom_call_target="tpu_custom_call" | custom-call | tf_op jit(solution)/shard_map/pallas_call | solution.py:730
  42.7 0.0 copy-done
  42.7 0.7 %broadcast_add_fusion = f32[47,256]{1,0:T(8,128)} fusion(f32[47,256]{1,0:T(8,128)S(1)} %shard_map.127, f32[47]{0:T(128)S(1)} %copy-done), kind=kLoop, calls=%fused_computation | loop fusion | flops 12032 | bytes 96444 | tf_op jit(solution)/shard_map/add | solution.py:796
Async XLA Ops:
  0.0 42.7 %copy-start = (f32[47]{0:T(128)S(1)}, f32[47]{0:T(128)}, u32[]{:S(2)}) copy-start(f32[47]{0:T(128)} %param.25) | copy-start | bytes 568

commit v5 on v4

--- a/solution.py
+++ b/solution.py
@@ -413,13 +413,13 @@
     put(send, send_rest, half + 1, pick(half + 1, 1))
     feature(peer(half), half, 0)
     put(send, send_rest, 1, pick(1, 0))
-    put(got, got_rest, 1, pick(0, 1))
     lax.fori_loop(2, half // 4, pick_and_send, 0)
     take(0)
     hand_on(1)[0].start()
     for k in range(1, 4):
         asked_for(half // 2, k).wait_recv()
         lax.fori_loop(k * half // 4, (k + 1) * half // 4, pick_and_send, 0)
+    put(got, got_rest, 1, pick(0, 1))
     asked_for(devices - 1, 0).wait_send()
     remote(req2_ref.at[rest], asked.at[rest], load_sems.at[1], in_sems.at[0], peer(1)).wait()
     onehot_slots(asked, onehot, cap_two, 0, 2)

time: 43.5 us -> 43.6 us (level)
  no operation moved by 1% of the time
where the time goes in v5:
time: 43.6 us; the launch traced here: 43.5 us
  Pallas kernels  42.7 us (98%)
  other arithmetic  0.7 us (2%)
    pallas_call x1, Pallas kernels, body(): pl.pallas_call(functools.partial(whole_kernel, lax.axis_size(AXES[1]), ro...  42.7 us

profile of v5, /device:TPU:0, one launch (start us, length us, event | category | flops | bytes accessed | tf_op | source)
XLA Modules:
  0.0 43.5 jit_solution(12590718581185362385)
XLA Ops:
  0.0 0.0 copy-start
  0.0 42.7 %shard_map.127 = f32[47,256]{1,0:T(8,128)S(1)} custom-call(bf16[100,19456]{1,0:T(8,128)(2,1)} %refs_0_.1, s32[32,1,128]{2,1,0:T(1,128)} %bitcast.7, s32[32,1,128]{2,1,0:T(1,128)} %bitcast.8, s32[32]{0:T(128)} %refs_3_.1, s32[32]{0:T(128)} %refs_4_.1, s32[11,1024]{1,0:T(8,128)} %refs_5_.1, s32[16,256]{1,0:T(8,128)} %refs_6_.1, bf16[100,256]{1,0:T(8,128)(2,1)} %bitcast.5, ...), custom_call_target="tpu_custom_call" | custom-call | tf_op jit(solution)/shard_map/pallas_call | solution.py:730
  42.8 0.0 copy-done
  42.8 0.7 %broadcast_add_fusion = f32[47,256]{1,0:T(8,128)} fusion(f32[47,256]{1,0:T(8,128)S(1)} %shard_map.127, f32[47]{0:T(128)S(1)} %copy-done), kind=kLoop, calls=%fused_computation | loop fusion | flops 12032 | bytes 96444 | tf_op jit(solution)/shard_map/add | solution.py:796
Async XLA Ops:
  0.0 42.8 %copy-start = (f32[47]{0:T(128)S(1)}, f32[47]{0:T(128)}, u32[]{:S(2)}) copy-start(f32[47]{0:T(128)} %param.25) | copy-start | bytes 568
